TPU v7x, 256 devices: a whole 4x4x8 slice. The times are simulated.
256 devices in a mesh: ctx: 128 (over x, y, z_lo, core), fsdp: 2 (over z_hi).
Axes of the slice: x: 4, y: 4, z: 8 (z_hi: 2, z_lo: 4; z = z_hi * 4 + z_lo), core: 2. Of those that a mesh axis runs over, the one named last changes fastest.
Arguments:
- layer_input: bfloat16 [16384, 4096], P('ctx'), may hold values from -8 to 8
- gain: float32 [4096], replicated, may hold values from 0.5 to 1.5
- codes: int32 [4096, 384], P('fsdp'), may hold values from -2147483648 to 2147483646
- column_scale_quantized: int32 [64, 3072], P('fsdp'), may hold values from 0 to 255
- block_second_scale: float32 [64], replicated, may hold values from 0.03 to 0.12
- query_down_map: bfloat16 [4096, 16], replicated, may hold values from -0.09375 to 0.09375
- query_up_map: bfloat16 [16, 2048], P(None, 'fsdp'), may hold values from -0.29882812 to 0.29882812
- token_document: int32 [16384], P('ctx'), may hold values from 0 to 3, as said below
- output_cotangent: bfloat16 [16384, 2048], P('ctx', 'fsdp'), may hold values from -0.059814453 to 0.059814453
Outputs:
- attn: bfloat16 [16384, 2048], P('ctx', 'fsdp')
- grad_a: float32 [4096, 16], replicated
- up_map_gradient: float32 [16, 2048], P(None, 'fsdp')
Inputs may be any that keep to these rules, and one draw needn't show every extreme that they name: token_document never falls along the sequence; each document has 1 to 12288 tokens and one has exactly 12288.
All inputs are finite; a program needn't handle non-finite values.
Results may differ from a plain program's by a relative error of at most 0.028.
Values may be sent and summed in bfloat16 or wider, within the bound.
A program may use at most 192 MiB of HBM per device.

v0:
```python
import math

import jax
import jax.numpy as jnp
from jax import lax
from jax.sharding import PartitionSpec as P

QUERY_HEADS = 16
KEY_VALUE_HEADS = 4
HEAD_SIZE = 128


NF4_LEVELS = [
    -1.0,
    -0.6961928009986877,
    -0.5250730514526367,
    -0.39491748809814453,
    -0.28444138169288635,
    -0.18477343022823334,
    -0.09105003625154495,
    0.0,
    0.07958029955625534,
    0.16093020141124725,
    0.24611230194568634,
    0.33791524171829224,
    0.44070982933044434,
    0.5626170039176941,
    0.7229568362236023,
    1.0,
]
ADAPTER_SCALE = 2.0
ROPE_BASE = 500000.0


def side_by_side(arrays, axis, dim, along):
    both = jnp.concatenate(arrays, axis=along)
    whole, at, outs = (lax.all_gather(both, axis, axis=dim, tiled=True), 0, [])
    for a in arrays:
        outs.append(lax.slice_in_dim(whole, at, at + a.shape[along], axis=along))
        at += a.shape[along]
    return tuple(outs)


def total_of_pieces(array, axis):
    return lax.all_gather(array, axis).sum(0)


def dequantize(packed, column_scale_quantized, block_second_scale):
    row_count = packed.shape[0]
    pieces = [jnp.bitwise_and(jnp.right_shift(packed, 4 * nibble), 15) for nibble in range(8)]
    unpacked = jnp.stack(pieces, axis=-1).reshape(row_count, packed.shape[1] * 8)
    levels = jnp.zeros(unpacked.shape, jnp.float32)
    for slot_code, level_value in enumerate(NF4_LEVELS):
        levels = levels + jnp.where(
            unpacked == slot_code, jnp.float32(level_value), jnp.float32(0.0)
        )
    absmax = (
        (column_scale_quantized.astype(jnp.float32) + 1.0) / 256.0 * block_second_scale[:, None]
    )
    scaled = levels.reshape(row_count // 64, 64, -1) * absmax[:, None, :]
    return scaled.reshape(row_count, -1).astype(jnp.bfloat16)


def rope_angles(positions):
    freqs = jnp.exp(
        jnp.arange(HEAD_SIZE // 2, dtype=jnp.float32) * (-2.0 * math.log(ROPE_BASE) / HEAD_SIZE)
    )
    angle = positions.astype(jnp.float32)[:, None] * freqs[None, :]
    cosine = jnp.concatenate([jnp.cos(angle), jnp.cos(angle)], axis=-1)
    sine = jnp.concatenate([jnp.sin(angle), jnp.sin(angle)], axis=-1)
    return (cosine, sine)


def apply_rotation(field, rotary_phases):
    cosine, sine = rotary_phases
    half = HEAD_SIZE // 2
    turned = jnp.concatenate([-field[..., half:], field[..., :half]], axis=-1)
    return field * cosine[:, None, :] + turned * sine[:, None, :]


def rotate_back(grads, rotary_phases):
    cosine, sine = rotary_phases
    half = HEAD_SIZE // 2
    scaled = grads * sine[:, None, :]
    turned = jnp.concatenate([-scaled[..., half:], scaled[..., :half]], axis=-1)
    return grads * cosine[:, None, :] - turned


def rms_norm(layer_input, gain):
    wide = layer_input.astype(jnp.float32)
    inverse = lax.rsqrt(jnp.mean(wide * wide, axis=-1, keepdims=True) + 1e-05)
    return (wide * inverse * gain[None, :]).astype(jnp.bfloat16)


def fresh_state(head_count, head_grouped, row_count):
    small = jnp.zeros((head_count, head_grouped, row_count), jnp.float32)
    large = jnp.zeros((head_count, head_grouped, row_count, HEAD_SIZE), jnp.float32)
    return (small - 1e30, small, small, large, large, large)


def on_device(
    layer_input,
    gain,
    codes,
    column_scale_quantized,
    block_second_scale,
    query_down_map,
    query_up_map,
    token_document,
    output_cotangent,
):
    row_count = layer_input.shape[0]
    group_total = lax.axis_size("fsdp")
    my_place = lax.axis_index("ctx")
    query_width = query_up_map.shape[1]
    heads_here = query_width // HEAD_SIZE
    key_value_heads = KEY_VALUE_HEADS // group_total
    kv_width = key_value_heads * HEAD_SIZE
    head_grouped = QUERY_HEADS // KEY_VALUE_HEADS
    soft_scale = 1.0 / math.sqrt(HEAD_SIZE)
    my_codes, my_scales = (
        lax.all_to_all(codes, "fsdp", split_axis=1, concat_axis=0, tiled=True),
        lax.all_to_all(column_scale_quantized, "fsdp", split_axis=1, concat_axis=0, tiled=True),
    )
    weight = dequantize(my_codes, my_scales, block_second_scale)
    input_normalized = rms_norm(layer_input, gain)
    projection_output = jnp.dot(input_normalized, weight, preferred_element_type=jnp.float32)
    rank_reduced = jnp.dot(
        input_normalized, query_down_map, preferred_element_type=jnp.float32
    ).astype(jnp.bfloat16)
    query_complete = projection_output[:, :query_width] + ADAPTER_SCALE * jnp.dot(
        rank_reduced, query_up_map, preferred_element_type=jnp.float32
    )
    positions = my_place * row_count + jnp.arange(row_count, dtype=jnp.int32)
    last_position = my_place * row_count + row_count - 1
    rotary_phases = rope_angles(positions)
    query_rows = apply_rotation(
        query_complete.reshape(row_count, heads_here, HEAD_SIZE), rotary_phases
    ).astype(jnp.bfloat16)
    key_rows = apply_rotation(
        projection_output[:, query_width : query_width + kv_width].reshape(
            row_count, key_value_heads, HEAD_SIZE
        ),
        rotary_phases,
    ).astype(jnp.bfloat16)
    value_rows = (
        projection_output[:, query_width + kv_width :]
        .reshape(row_count, key_value_heads, HEAD_SIZE)
        .astype(jnp.bfloat16)
    )
    query_grouped = query_rows.reshape(row_count, key_value_heads, head_grouped, HEAD_SIZE)
    grouped_gradient = output_cotangent.reshape(row_count, key_value_heads, head_grouped, HEAD_SIZE)
    all_ids = lax.all_gather(token_document, "ctx", axis=0, tiled=True)

    def update(state, query_part, grad_part, key_part, value_part, key_start):
        key_count = key_part.shape[0]
        key_pos = key_start + jnp.arange(key_count, dtype=jnp.int32)
        key_ids = lax.dynamic_slice_in_dim(all_ids, key_start, key_count, 0)
        allowed = (token_document[:, None] == key_ids[None, :]) & (
            key_pos[None, :] <= positions[:, None]
        )

        def work(carry):
            run_max, run_sum, run_dot, run_out, run_grad, run_key = carry
            scores = (
                jnp.einsum(
                    "qhgd,khd->hgqk", query_part, key_part, preferred_element_type=jnp.float32
                )
                * soft_scale
            )
            masked = jnp.where(allowed, scores, -1e30)
            new_max = jnp.maximum(run_max, jnp.max(masked, axis=-1))
            expo = jnp.where(allowed, jnp.exp(masked - new_max[..., None]), 0.0)
            decay = jnp.exp(run_max - new_max)
            grad_dots = jnp.einsum(
                "qhgd,khd->hgqk", grad_part, value_part, preferred_element_type=jnp.float32
            )
            weighted = expo * grad_dots
            expo_low = expo.astype(jnp.bfloat16)
            run_sum = decay * run_sum + jnp.sum(expo, axis=-1)
            run_dot = decay * run_dot + jnp.sum(weighted, axis=-1)
            run_out = decay[..., None] * run_out + jnp.einsum(
                "hgqk,khd->hgqd", expo_low, value_part, preferred_element_type=jnp.float32
            )
            run_key = decay[..., None] * run_key + jnp.einsum(
                "hgqk,khd->hgqd", expo_low, key_part, preferred_element_type=jnp.float32
            )
            run_grad = decay[..., None] * run_grad + jnp.einsum(
                "hgqk,khd->hgqd",
                weighted.astype(jnp.bfloat16),
                key_part,
                preferred_element_type=jnp.float32,
            )
            return (new_max, run_sum, run_dot, run_out, run_grad, run_key)

        def unchanged(carry):
            return carry

        active = key_start <= last_position
        return lax.cond(active, work, unchanged, state)

    start_state = fresh_state(key_value_heads, head_grouped, row_count)
    key_piece, value_piece = side_by_side((key_rows, value_rows), "ctx", 0, 1)
    piece_len = key_piece.shape[0]
    key_block = math.gcd(piece_len, max(row_count, 512))
    block_count = piece_len // key_block

    def inner_block(number, carried):
        offset = number * key_block
        key_part = lax.dynamic_slice_in_dim(key_piece, offset, key_block, 0)
        value_part = lax.dynamic_slice_in_dim(value_piece, offset, key_block, 0)
        return update(carried, query_grouped, grouped_gradient, key_part, value_part, offset)

    state = lax.fori_loop(0, block_count, inner_block, start_state)
    run_max, run_sum, run_dot, run_out, run_grad, run_key = state
    output = run_out / run_sum[..., None]
    attn = jnp.transpose(output, (2, 0, 1, 3)).reshape(row_count, query_width).astype(jnp.bfloat16)
    mean_dot = run_dot / run_sum
    grad_query = soft_scale * (run_grad - mean_dot[..., None] * run_key) / run_sum[..., None]
    grad_query = jnp.transpose(grad_query, (2, 0, 1, 3)).reshape(row_count, heads_here, HEAD_SIZE)
    linear_gradient = (
        rotate_back(grad_query, rotary_phases).reshape(row_count, query_width).astype(jnp.bfloat16)
    )
    local_up_map = ADAPTER_SCALE * jnp.dot(
        rank_reduced.T, linear_gradient, preferred_element_type=jnp.float32
    )
    middle_gradient = (
        ADAPTER_SCALE * jnp.dot(linear_gradient, query_up_map.T, preferred_element_type=jnp.float32)
    ).astype(jnp.bfloat16)
    local_a = jnp.dot(input_normalized.T, middle_gradient, preferred_element_type=jnp.float32)
    up_map_gradient = total_of_pieces(local_up_map, "ctx")
    grad_a = lax.psum(local_a, ("ctx", "fsdp"))
    return (attn, grad_a, up_map_gradient)


def solution(mesh):
    return jax.shard_map(
        on_device,
        mesh=mesh,
        in_specs=(
            P("ctx", None),
            P(),
            P("fsdp", None),
            P("fsdp", None),
            P(),
            P(),
            P(None, "fsdp"),
            P("ctx"),
            P("ctx", "fsdp"),
        ),
        out_specs=(P("ctx", "fsdp"), P(), P(None, "fsdp")),
        check_vma=False,
    )
```

profile of v0, /device:TPU:1, one launch (start us, length us, event | category | flops | bytes accessed | tf_op | source)
XLA Modules:
  0.0 1287.0 jit_solution(3641267997572594899)
XLA Ops:
  7.2 1.8 copy.169
  9.0 9.0 all-to-all-start.1
  18.0 3.6 copy.121
  21.6 6.0 all-to-all-done.1
  27.6 0.7 copy-done.13
  28.3 3.9 all-to-all-start
  32.7 0.5 copy-done.15
  33.3 1.5 fusion.27
  34.9 1.0 convert_add_fusion
  35.9 0.8 bitcast_multiply_fusion.4
  36.7 12.5 mul.234
  49.3 25.3 %copy.132 = f32[4096,1536]{0,1:T(8,128)} copy(f32[4096,1536]{1,0:T(8,128)} %bitcast.142) | data formatting | bytes 50331648 | tf_op jit(solution)/shard_map/mul | solution.py:60
  74.5 7.5 and_bitcast_fusion
  82.1 4.1 copy.122
  86.2 5.8 and.142
  92.0 3.8 constant_dynamic-update-slice_fusion.7
  95.8 4.1 copy.123
  99.9 5.6 and.145
  105.5 6.1 copy.124
  111.7 5.8 and.148
  117.4 4.1 copy.125
  121.5 5.6 and.151
  127.2 6.1 copy.126
  133.3 5.6 and.154
  138.9 4.1 copy.127
  143.0 5.8 and.157
  148.8 6.1 copy.128
  155.0 5.6 and.160
  160.6 4.1 copy.129
  164.7 5.7 and.163
  170.4 1.9 constant_dynamic-update-slice_fusion.6
  172.3 1.1 copy-done.6
  173.5 1.8 constant_dynamic-update-slice_fusion.5
  175.3 1.9 constant_dynamic-update-slice_fusion.4
  177.2 1.8 constant_dynamic-update-slice_fusion.3
  179.0 1.9 constant_dynamic-update-slice_fusion.2
  180.9 0.5 copy-done.10
  181.5 2.0 constant_dynamic-update-slice_fusion.1
  183.4 1.9 constant_dynamic-update-slice_fusion
  185.3 38.7 %add_add_fusion = f32[4096,192,8]{0,1,2:T(8,128)} fusion(s32[4096,192,8]{0,1,2:T(8,128)} %constant_dynamic-update-slice_fusion), kind=kLoop, calls=%fused_computation.35 | loop fusion | flops 276824064 | bytes 50331648 | tf_op jit(solution)/shard_map/add | solution.py:54
  224.0 27.1 %fusion.25 = f32[128,1536]{1,0:T(8,128)S(1)} fusion(f32[4096,1536]{0,1:T(8,128)} %copy.132, f32[4096,192,8]{0,1,2:T(8,128)} %add_add_fusion, bf16[128,4096]{1,0:T(8,128)(2,1)S(1)} %copy-done.12, f32[4096]{0:T(1024)S(1)} %copy-done.20, f32[128]{0:T(128)S(1)} %add_rsqrt_fusion), kind=kOutput, calls=%fused_computation.36 | convolution fusion | flops 1625292800 | bytes 52183552 | tf_op jit(solution)/shard_map/dot_general | solution.py:127
  251.4 0.7 pad_maximum_fusion.1
  252.3 0.9 copy.146
  253.2 218.5 %all-gather.1 = s32[128,1,128]{2,1,0:T(1,128)S(1)} all-gather(s32[1,1,128]{2,1,0:T(1,128)S(1)} %bitcast.164), channel_id=1, replica_groups=mesh['ctx'=128,'fsdp'=2] {'ctx'}, dimensions={0}, use_global_device_ids=true | all-gather | bytes 66048 | tf_op jit(solution)/shard_map/all_gather | solution.py:153
  471.7 0.4 convolution_convert_fusion
  473.6 22.6 %all-gather.5.cloned.1.call-done = bf16[16384,4,128]{2,0,1:T(8,128)(2,1)} async-done(((bf16[128,4,128]{2,0,1:T(8,128)(2,1)}), bf16[16384,4,128]{2,0,1:T(8,128)(2,1)}) %all-gather.5.cloned.1.call-update) | async-done | bytes 16777232 | tf_op jit(solution)/shard_map/all_gather | solution.py:37
  496.3 11.5 fusion.46
  507.9 11.9 while.24
  507.9 9.6 conditional.3
  508.3 1.4 fusion.2
  509.7 1.8 fusion.45
  511.5 1.9 convolution_add_fusion
  513.4 1.7 convolution_add_fusion.1
  515.1 1.9 convolution_add_fusion.2
  517.0 0.5 fusion.5
  520.5 0.9 bitcast_multiply_fusion.2
  521.5 1.0 fusion.36
  522.5 0.8 convolution_multiply_fusion.1
  523.4 1.9 fusion.32
  525.4 0.9 copy.150
  526.2 495.8 %all-gather.7.cloned.1.call-done = f32[2048,1024]{1,0:T(8,128)} async-done(((f32[16,1024]{1,0:T(8,128)}), f32[2048,1024]{1,0:T(8,128)}) %all-gather.7.cloned.1.call-update) | async-done | bytes 8388624 | tf_op jit(solution)/shard_map/all_gather | solution.py:45
  1022.1 4.5 reduce_sum.43
  1026.5 252.1 %all-reduce.2.cloned.1.call-done = f32[4096,16]{0,1:T(8,128)} async-done(((f32[4096,16]{0,1:T(8,128)}), f32[4096,16]{0,1:T(8,128)}) %all-reduce.2.cloned.1.call-update) | async-done | bytes 262160 | tf_op jit(solution)/shard_map/psum | solution.py:232
  1278.7 1.7 copy.214
  (187 shorter events, 4.5 us)
Async XLA Ops:
  7.2 464.5 %copy-start = (bf16[4096,16]{0,1:T(8,128)(2,1)S(1)}, bf16[4096,16]{0,1:T(8,128)(2,1)}, u32[]{:S(2)}) copy-start(bf16[4096,16]{0,1:T(8,128)(2,1)} %param.18) | copy-start | bytes 393220
  9.0 18.6 %all-to-all-start.1 = ((s32[32,2,1536]{2,0,1:T(8,128)}), s32[32,2,1536]{2,0,1:T(8,128)S(1)}, u32[]{:S(2)}, u32[]{:S(2)}) async-start(s32[32,2,1536]{2,0,1:T(8,128)} %bitcast.131), calls=%async_computation.1 | async-start | bytes 786432 | tf_op jit(solution)/shard_map/all_to_all | solution.py:123
  18.0 16.9 %copy-start.23 = (f32[64]{0:T(128)S(1)}, f32[64]{0:T(128)}, u32[]{:S(2)}) copy-start(f32[64]{0:T(128)} %param.17) | copy-start | bytes 772
  27.6 0.7 copy-start.13
  28.3 46.2 %all-to-all-start = ((s32[2048,2,192]{0,2,1:T(8,128)}), s32[2048,2,192]{0,2,1:T(8,128)S(1)}, u32[]{:S(2)}, u32[]{:S(2)}) async-start(s32[2048,2,192]{0,2,1:T(8,128)} %bitcast.143), calls=%async_computation | async-start | bytes 6291456 | tf_op jit(solution)/shard_map/all_to_all | solution.py:122
  32.3 464.0 %all-gather.5.cloned.1.call-start = ((), (), s32[]{:S(2)}) async-start(), calls=%async_computation.2 | async-start | bytes 16908288 | tf_op jit(solution)/shard_map/all_gather | solution.py:37
  32.6 0.6 copy-start.15
  32.6 16.7 %copy-start.14 = (f32[128,128]{0,1:T(8,128)}, f32[128,128]{0,1:T(8,128)S(1)}, u32[]{:S(2)}) copy-start(f32[128,128]{0,1:T(8,128)S(1)} %get-tuple-element.631) | copy-start | bytes 196612
  34.9 436.9 %copy-start.21 = (f32[128]{0:T(128)}, f32[128]{0:T(128)S(1)}, u32[]{:S(2)}) copy-start(f32[128]{0:T(128)S(1)} %add_rsqrt_fusion) | copy-start | bytes 1540
  86.2 9.7 copy-start.4
  105.5 11.9 copy-start.3
  127.2 11.8 copy-start.2
  148.8 11.8 copy-start.1
  164.7 5.7 copy-start.5
  170.4 3.0 copy-start.6
  170.4 4.9 copy-start.7
  173.5 3.7 copy-start.8
  175.3 3.7 copy-start.9
  177.2 4.3 copy-start.10
  179.0 4.4 copy-start.11
  185.3 38.7 %copy-start.12 = (bf16[128,4096]{1,0:T(8,128)(2,1)S(1)}, bf16[128,4096]{1,0:T(8,128)(2,1)}, u32[]{:S(2)}) copy-start(bf16[128,4096]{1,0:T(8,128)(2,1)} %param.13) | copy-start | bytes 3145732
  185.3 38.7 %copy-start.20 = (f32[4096]{0:T(1024)S(1)}, f32[4096]{0:T(1024)}, u32[]{:S(2)}) copy-start(f32[4096]{0:T(1024)} %param.14) | copy-start | bytes 49156
  224.0 28.2 %copy-start.16 = (bf16[128,1024]{1,0:T(8,128)(2,1)S(1)}, bf16[128,1024]{1,0:T(8,128)(2,1)}, u32[]{:S(2)}) copy-start(bf16[128,1024]{1,0:T(8,128)(2,1)} %param.21) | copy-start | bytes 786436
  224.0 29.2 %copy-start.19 = (s32[128]{0:T(128)S(1)}, s32[128]{0:T(128)}, u32[]{:S(2)}) copy-start(s32[128]{0:T(128)} %param.20) | copy-start | bytes 1540
  224.0 248.2 %copy-start.18 = (bf16[16,1024]{1,0:T(8,128)(2,1)S(1)}, bf16[16,1024]{1,0:T(8,128)(2,1)}, u32[]{:S(2)}) copy-start(bf16[16,1024]{1,0:T(8,128)(2,1)} %param.19) | copy-start | bytes 98308
  252.1 769.9 %all-gather.7.cloned.1.call-start = ((), (), s32[]{:S(2)}) async-start(), calls=%async_computation.4 | async-start | bytes 8454144 | tf_op jit(solution)/shard_map/all_gather | solution.py:45
  473.6 34.3 %copy-start.17 = (bf16[128,2,4,128]{3,0,2,1:T(8,128)(2,1)S(1)}, bf16[128,2,4,128]{3,0,2,1:T(8,128)(2,1)}, u32[]{:S(2)}) copy-start(bf16[128,2,4,128]{3,0,2,1:T(8,128)(2,1)} %copy.146) | copy-start | bytes 786436
  519.8 3.6 copy-start.22
  523.4 755.3 %all-reduce.2.cloned.1.call-start = ((), (), s32[]{:S(2)}) async-start(), calls=%async_computation.3 | async-start | bytes 524288 | tf_op jit(solution)/shard_map/psum | solution.py:232
Sparse Core Ops, SparseCore 0:
  252.2 243.9 all-gather.4
  523.5 498.5 all-gather.6
  1028.1 250.5 all-reduce.1
where the time goes:
time: 1300 us; the launch traced here: 1290 us
  waiting for transfers between devices  777 us (60%)
  blocking collectives  219 us (17%)
  local copies, waits for them, and re-layouts  165 us (13%)
  other arithmetic  58.3 us (4%)
  matrix products  39.3 us (3%)
  between operations  14.4 us (1%)
  starting transfers between devices  13.1 us (1%)
    all_gather x1, waiting for transfers between devices, total_of_pieces(): return lax.all_gather(array, axis).sum(0)  496 us
    psum x1, waiting for transfers between devices, on_device(): grad_a = lax.psum(local_a, ('ctx', 'fsdp'))  252 us
    all_gather x1, blocking collectives, on_device(): all_ids = lax.all_gather(token_document, 'ctx', axis=0, tiled=True)  219 us
    and x16, local copies, waits for them, and re-layouts, dequantize(): jnp.bitwise_and(jnp.right_shift(packed, 4 * nibble), 15)  84.5 us
    add x1, other arithmetic, dequantize(): levels + jnp.where(unpacked == slot_code, jnp.float32(level_value), jnp.f...  38.7 us
    mul x2, local copies, waits for them, and re-layouts, dequantize(): scaled = levels.reshape(row_count // 64, 64, -1) * absmax[:, None, :]  37.8 us
    dot_general x1, matrix products, on_device(): jnp.dot(input_normalized, weight, preferred_element_type=jnp.float32)  27.1 us
  transfers between devices with their start and end apart: 5, of which 4 were waited for; matrix products, arithmetic and copies ran while one was open for 4% of the time, Pallas kernels for 0%

commit v1 on v0

v1 whole, which is shorter than its diff:
```python
import functools
import math

import jax
import jax.numpy as jnp
from jax import lax
from jax.experimental import pallas as pl
from jax.experimental.pallas import tpu as pltpu
from jax.sharding import PartitionSpec as P

MESH = pl.DeviceIdType.MESH
HEAD = 128
NF4_LEVELS = [
    -1.0,
    -0.6961928009986877,
    -0.5250730514526367,
    -0.39491748809814453,
    -0.28444138169288635,
    -0.18477343022823334,
    -0.09105003625154495,
    0.0,
    0.07958029955625534,
    0.16093020141124725,
    0.24611230194568634,
    0.33791524171829224,
    0.44070982933044434,
    0.5626170039176941,
    0.7229568362236023,
    1.0,
]
ADAPTER_SCALE = 2.0
ROPE_BASE = 500000.0
SOFT_SCALE = 1.0 / math.sqrt(HEAD)
QUERY_SCALE = SOFT_SCALE * math.log2(math.e)
F32, BF16, I32 = jnp.float32, jnp.bfloat16, jnp.int32
VMEM_LIMIT = 60 * 1024 * 1024


def places():
    c = lax.axis_index("ctx")
    f = lax.axis_index("fsdp")
    return c // 32, (c // 8) % 4, (c // 2) % 4, c % 2, f


def ctx_of(x, y, z, j):
    return ((x * 4 + y) * 4 + z) * 2 + j


def lookup(table, index):
    return lax.gather(
        table,
        index[..., None],
        lax.GatherDimensionNumbers(
            offset_dims=(),
            collapsed_slice_dims=(1,),
            start_index_map=(1,),
            operand_batching_dims=(0,),
            start_indices_batching_dims=(0,),
        ),
        slice_sizes=(1, 1),
        mode=lax.GatherScatterMode.PROMISE_IN_BOUNDS,
    )


def remote(src, dst, send, recv, ctx, f):
    return pltpu.make_async_remote_copy(
        src_ref=src, dst_ref=dst, send_sem=send, recv_sem=recv, device_id=(ctx, f), device_id_type=MESH
    )


def project_kernel(
    x_ref, gain_ref, codes_ref, sq_ref, bs_ref, downt_ref, up_ref, cos_ref, sin_ref, table_ref,
    q_ref, kv_ref, normed_ref, lowt_ref,
    perm, scale, w_buf, acc, nat, send_main, send_half, recv_main, recv_half, total, send_sem, recv_sem,
):
    c = lax.axis_index("ctx")
    f = lax.axis_index("fsdp")
    other = 1 - f
    barrier = pltpu.get_barrier_semaphore()
    pl.semaphore_signal(barrier, inc=1, device_id=(c, other), device_id_type=MESH)

    wide = x_ref[...].astype(F32)
    inverse = lax.rsqrt(jnp.mean(wide * wide, axis=-1, keepdims=True) + 1e-05)
    normed_ref[...] = (wide * inverse * gain_ref[...]).astype(BF16)

    for part in range(8):
        m = lax.broadcasted_iota(I32, (128, 1024), 0)
        k = lax.broadcasted_iota(I32, (128, 1024), 1)
        perm[128 * part : 128 * part + 128, :] = jnp.where(k == 8 * m + part, 1.0, 0.0).astype(BF16)
    second = bs_ref[pl.ds(pl.multiple_of(32 * f, 32), 32), :] * (1.0 / 256.0)
    for t in range(3):
        quantized = (sq_ref[:, 1024 * t : 1024 * t + 1024].astype(F32) + 1.0).astype(BF16)
        packed = lax.dot_general(quantized, perm[...], (((1,), (1,)), ((), ())), preferred_element_type=F32)
        scale[t] = packed * second

    table = jnp.broadcast_to(table_ref[...], (64, 128))

    def tile(t):
        lane = pl.multiple_of(t * 128, 128)
        acc[...] = jnp.zeros_like(acc)

        def chunk(kc, carry):
            for b in range(4):
                row = pl.multiple_of(kc * 256 + b * 64, 64)
                words = codes_ref[pl.ds(row, 64), pl.ds(lane, 128)]
                scale_row = scale[t, pl.ds(kc * 4 + b, 1), :]
                for n in range(8):
                    index = jnp.bitwise_and(jnp.right_shift(words, 4 * n), 15)
                    levels = lookup(table, index)
                    w_buf[64 * b : 64 * b + 64, 128 * n : 128 * n + 128] = (
                        levels * scale_row[:, 128 * n : 128 * n + 128]
                    ).astype(BF16)
            col = pl.multiple_of(f * 2048 + kc * 256, 256)
            acc[...] += jnp.dot(normed_ref[:, pl.ds(col, 256)], w_buf[...], preferred_element_type=F32)
            return carry

        lax.fori_loop(0, 8, chunk, 0)
        full = acc[...]
        high = full.astype(BF16)
        low = (full - high.astype(F32)).astype(BF16)
        nat[...] = jnp.dot(high, perm[...], preferred_element_type=F32) + jnp.dot(
            low, perm[...], preferred_element_type=F32
        )

    own_main = pl.ds(pl.multiple_of(512 * f, 512), 1024)
    own_half = pl.ds(pl.multiple_of(1024 * (1 - f), 512), 512)

    tile(2 * (1 - f))
    send_main[...] = nat[...].astype(BF16)
    pl.semaphore_wait(barrier, 1)
    copy_main = remote(send_main, recv_main, send_sem.at[0], recv_sem.at[0], c, other)
    copy_main.start()
    tile(1)
    send_half[...] = nat[:, pl.ds(pl.multiple_of(512 * (1 - f), 512), 512)].astype(BF16)
    copy_half = remote(send_half, recv_half, send_sem.at[1], recv_sem.at[1], c, other)
    copy_half.start()
    total[:, own_half] = nat[:, pl.ds(pl.multiple_of(512 * f, 512), 512)]
    tile(2 * f)
    total[:, own_main] = nat[...]

    lowt = lax.dot_general(
        downt_ref[...], normed_ref[...], (((1,), (1,)), ((), ())), preferred_element_type=F32
    ).astype(BF16)
    lowt_ref[...] = lowt
    nat[...] = ADAPTER_SCALE * lax.dot_general(
        lowt, up_ref[...], (((0,), (0,)), ((), ())), preferred_element_type=F32
    )

    copy_main.wait()
    total[:, own_main] += recv_main[...].astype(F32)
    copy_half.wait()
    total[:, own_half] += recv_half[...].astype(F32)

    cosine, sine = cos_ref[...], sin_ref[...]

    def rotate(v):
        return v * cosine + pltpu.roll(v, 64, 1) * sine

    for h in range(8):
        s = slice(128 * h, 128 * h + 128)
        q_ref[:, s] = (rotate(total[:, s] + nat[:, s]) * QUERY_SCALE).astype(BF16)
    for h in range(2):
        kv_ref[h, :, 0:128] = rotate(total[:, 1024 + 128 * h : 1152 + 128 * h]).astype(BF16)
        kv_ref[h, :, 128:256] = total[:, 1280 + 128 * h : 1408 + 128 * h].astype(BF16)


def project(x, gain, codes, sq, bs, downt, up, cosine, sine, table):
    vmem = pl.BlockSpec(memory_space=pltpu.VMEM)
    return pl.pallas_call(
        project_kernel,
        name="project",
        out_shape=(
            jax.ShapeDtypeStruct((128, 1024), BF16),
            jax.ShapeDtypeStruct((2, 128, 256), BF16),
            jax.ShapeDtypeStruct((128, 4096), BF16),
            jax.ShapeDtypeStruct((16, 128), BF16),
        ),
        in_specs=[vmem] * 10,
        out_specs=(vmem,) * 4,
        scratch_shapes=[
            pltpu.VMEM((1024, 1024), BF16),
            pltpu.VMEM((3, 32, 1024), F32),
            pltpu.VMEM((256, 1024), BF16),
            pltpu.VMEM((128, 1024), F32),
            pltpu.VMEM((128, 1024), F32),
            pltpu.VMEM((128, 1024), BF16),
            pltpu.VMEM((128, 512), BF16),
            pltpu.VMEM((128, 1024), BF16),
            pltpu.VMEM((128, 512), BF16),
            pltpu.VMEM((128, 1536), F32),
            pltpu.SemaphoreType.DMA((2,)),
            pltpu.SemaphoreType.DMA((2,)),
        ],
        compiler_params=pltpu.CompilerParams(
            collective_id=0, has_side_effects=True, vmem_limit_bytes=VMEM_LIMIT
        ),
    )(x, gain, codes, sq, bs, downt, up, cosine, sine, table)


def gather_kernel(
    q_ref, kv_ref, do_ref, lowt_ref, ids_ref,
    qx, dox, kvg, idg, lowx,
    pair_send, pair_recv, own_sem, z_send, z_recv, zi_send, zi_recv, a_send, a_recv, ai_send, ai_recv,
    b_send, b_recv, bi_send, bi_recv,
):
    x, y, z, j, f = places()
    i = 1 - j
    u = x * i + y * j
    v = y * i + x * j

    def at(uu, vv, zz):
        return ctx_of(uu * i + vv * j, vv * i + uu * j, zz, j)

    def slot(uu, vv, zz):
        return (uu * 4 + vv) * 4 + zz

    sibling = ctx_of(x, y, z, i)
    vr, vl, vo = (v + 1) % 4, (v + 3) % 4, (v + 2) % 4
    ur, ul, uo = (u + 1) % 4, (u + 3) % 4, (u + 2) % 4
    right_v, left_v = at(u, vr, z), at(u, vl, z)
    right_u, left_u = at(ur, v, z), at(ul, v, z)

    barrier = pltpu.get_barrier_semaphore()
    peers = [sibling, right_v, left_v, right_u, left_u] + [at(u, v, (z + d) % 4) for d in (1, 2, 3)]
    for peer in peers:
        pl.semaphore_signal(barrier, inc=1, device_id=(peer, f), device_id_type=MESH)
    pl.semaphore_wait(barrier, len(peers))

    mine = slot(u, v, z)
    theirs = slot(v, u, z)
    near = pl.ds(pl.multiple_of(512 * j, 512), 512)
    far = pl.ds(pl.multiple_of(512 * i, 512), 512)
    pairs = [
        (kv_ref.at[i], kvg.at[theirs, j]),
        (ids_ref, idg.at[theirs, j]),
        (q_ref.at[:, far], qx.at[j]),
        (do_ref.at[:, far], dox.at[j]),
        (lowt_ref, lowx.at[j]),
    ]
    sent = []
    for n, (src, dst) in enumerate(pairs):
        copy = remote(src, dst, pair_send.at[n], pair_recv.at[n], sibling, f)
        copy.start()
        sent.append(copy)
    own = [
        (kv_ref.at[j], kvg.at[mine, j]),
        (ids_ref, idg.at[mine, j]),
        (q_ref.at[:, near], qx.at[j]),
        (do_ref.at[:, near], dox.at[j]),
        (lowt_ref, lowx.at[j]),
    ]
    local = []
    for n, (src, dst) in enumerate(own):
        copy = pltpu.make_async_copy(src, dst, own_sem.at[n])
        copy.start()
        local.append(copy)

    def arrived(ref, send, recv):
        remote(ref, ref, send, recv, sibling, f).wait_recv()

    arrived(kvg.at[mine, i], pair_send.at[0], pair_recv.at[0])
    arrived(idg.at[mine, i], pair_send.at[1], pair_recv.at[1])
    local[0].wait()
    local[1].wait()

    for d in (1, 2, 3):
        peer = at(u, v, (z + d) % 4)
        for ref, send, recv in ((kvg, z_send, z_recv), (idg, zi_send, zi_recv)):
            copy = remote(ref.at[mine], ref.at[mine], send.at[d - 1], recv.at[d - 1], peer, f)
            copy.start()
            sent.append(copy)
    for d in (1, 2, 3):
        source = slot(u, v, (z + 4 - d) % 4)
        arrived(kvg.at[source], z_send.at[d - 1], z_recv.at[d - 1])
        arrived(idg.at[source], zi_send.at[d - 1], zi_recv.at[d - 1])

    def half(vv, h):
        return pl.ds(slot(u, vv, 0) + 2 * h, 2)

    def whole(vv):
        return pl.ds(slot(u, vv, 0), 4)

    def piece(uu, vv):
        return pl.ds(slot(uu, vv, 0), 4)

    def push(part, n, send, recv, peer, ref=kvg):
        copy = remote(ref.at[part], ref.at[part], send.at[n], recv.at[n], peer, f)
        copy.start()
        sent.append(copy)

    def got(part, n, send, recv, ref=kvg):
        arrived(ref.at[part], send.at[n], recv.at[n])

    push(half(v, 0), 0, a_send, a_recv, right_v)
    push(half(v, 1), 3, a_send, a_recv, left_v)
    push(half(v, 1), 1, a_send, a_recv, right_v)
    push(half(v, 0), 4, a_send, a_recv, left_v)
    push(whole(v), 0, ai_send, ai_recv, right_v, idg)
    push(whole(v), 1, ai_send, ai_recv, left_v, idg)
    push(piece(u, v), 0, b_send, b_recv, right_u)
    push(piece(u, v), 4, b_send, b_recv, left_u)
    got(half(vl, 0), 0, a_send, a_recv)
    push(half(vl, 0), 2, a_send, a_recv, right_v)
    got(half(vr, 1), 3, a_send, a_recv)
    push(half(vr, 1), 5, a_send, a_recv, left_v)
    got(half(vl, 1), 1, a_send, a_recv)
    got(whole(vl), 0, ai_send, ai_recv, idg)
    push(whole(vl), 2, ai_send, ai_recv, right_v, idg)
    push(piece(u, vl), 1, b_send, b_recv, right_u)
    push(piece(u, vl), 5, b_send, b_recv, left_u)
    got(half(vr, 0), 4, a_send, a_recv)
    got(whole(vr), 1, ai_send, ai_recv, idg)
    push(piece(u, vr), 2, b_send, b_recv, right_u)
    push(piece(u, vr), 6, b_send, b_recv, left_u)
    got(half(vo, 0), 2, a_send, a_recv)
    got(half(vo, 1), 5, a_send, a_recv)
    got(whole(vo), 2, ai_send, ai_recv, idg)
    push(piece(u, vo), 3, b_send, b_recv, right_u)
    push(piece(u, vo), 7, b_send, b_recv, left_u)

    def all_of(uu):
        return pl.ds(slot(uu, 0, 0), 16)

    push(all_of(u), 0, bi_send, bi_recv, right_u, idg)
    push(all_of(u), 1, bi_send, bi_recv, left_u, idg)

    got(piece(ul, v), 0, b_send, b_recv)
    push(piece(ul, v), 8, b_send, b_recv, right_u)
    got(piece(ul, vl), 1, b_send, b_recv)
    push(piece(ul, vl), 9, b_send, b_recv, right_u)
    got(piece(ur, vr), 6, b_send, b_recv)
    push(piece(ur, vr), 10, b_send, b_recv, left_u)
    got(piece(ur, vo), 7, b_send, b_recv)
    push(piece(ur, vo), 11, b_send, b_recv, left_u)
    got(all_of(ul), 0, bi_send, bi_recv, idg)
    push(all_of(ul), 2, bi_send, bi_recv, right_u, idg)
    got(all_of(ur), 1, bi_send, bi_recv, idg)
    got(piece(ul, vr), 2, b_send, b_recv)
    got(piece(ul, vo), 3, b_send, b_recv)
    got(piece(ur, v), 4, b_send, b_recv)
    got(piece(ur, vl), 5, b_send, b_recv)
    got(piece(uo, v), 8, b_send, b_recv)
    got(piece(uo, vl), 9, b_send, b_recv)
    got(piece(uo, vr), 10, b_send, b_recv)
    got(piece(uo, vo), 11, b_send, b_recv)
    got(all_of(uo), 2, bi_send, bi_recv, idg)

    arrived(qx.at[i], pair_send.at[2], pair_recv.at[2])
    arrived(dox.at[i], pair_send.at[3], pair_recv.at[3])
    arrived(lowx.at[i], pair_send.at[4], pair_recv.at[4])
    for copy in local[2:]:
        copy.wait()
    for copy in sent:
        copy.wait_send()


def gather(q, kv, do, lowt, ids):
    vmem = pl.BlockSpec(memory_space=pltpu.VMEM)
    hbm = pl.BlockSpec(memory_space=pl.ANY)
    dma = pltpu.SemaphoreType.DMA
    counts = (5, 5, 5, 3, 3, 3, 3, 6, 6, 3, 3, 12, 12, 3, 3)
    return pl.pallas_call(
        gather_kernel,
        name="gather",
        out_shape=(
            jax.ShapeDtypeStruct((2, 128, 512), BF16),
            jax.ShapeDtypeStruct((2, 128, 512), BF16),
            jax.ShapeDtypeStruct((64, 2, 128, 256), BF16),
            jax.ShapeDtypeStruct((64, 2, 8, 128), I32),
            jax.ShapeDtypeStruct((2, 16, 128), BF16),
        ),
        in_specs=[vmem] * 5,
        out_specs=(hbm,) * 5,
        scratch_shapes=[dma((n,)) for n in counts],
        compiler_params=pltpu.CompilerParams(
            collective_id=1, has_side_effects=True, vmem_limit_bytes=VMEM_LIMIT
        ),
    )(q, kv, do, lowt, ids)


def attend_kernel(
    qx_ref, dox_ref, kvg_ref, idg_ref, cos_ref, sin_ref, ox_ref, glx_ref, qt, dot_, run_max, run_sum, acc, acc2
):
    x, y, z, j, _ = places()
    chip = (x * 4 + y) * 4 + z

    def slot(number):
        a, b, d = number // 16, (number // 4) % 4, number % 4
        return jnp.where(j == 0, (a * 4 + b) * 4 + d, (b * 4 + a) * 4 + d)

    here = slot(chip)
    ids = jnp.concatenate([idg_ref[here, 0, 0:1, :], idg_ref[here, 1, 0:1, :]], axis=1)
    every = idg_ref[...].reshape(128, 8, 128)
    start = jnp.zeros((1, 256), I32)
    for d in (1, 2, 3):
        below = jnp.sum(jnp.sum(jnp.where(every < d, 1, 0), axis=0), axis=1, keepdims=True)[0:1, :]
        start = jnp.where(ids == d, below, start)
    first = jnp.min(start) // 256
    position = chip * 256 + lax.broadcasted_iota(I32, (1, 256), 1)

    for g in range(4):
        lanes = slice(128 * g, 128 * g + 128)
        for b in range(2):
            cols = slice(256 * g + 128 * b, 256 * g + 128 * b + 128)
            qt[:, cols] = qx_ref[b, :, lanes].T
            dot_[:, cols] = dox_ref[b, :, lanes].T
    run_max[...] = jnp.full_like(run_max, -1e29)
    run_sum[...] = jnp.zeros_like(run_sum)
    acc[...] = jnp.zeros_like(acc)
    acc2[...] = jnp.zeros_like(acc2)

    def chunk(number, carry):
        at = slot(number)
        kv = jnp.concatenate([kvg_ref[at, 0], kvg_ref[at, 1]], axis=0)
        kvt = kv.T
        keys, values = kv[:, :128], kv[:, 128:]
        key_pos = number * 256 + lax.broadcasted_iota(I32, (256, 256), 0)
        allowed = (key_pos >= start) & (key_pos <= position)
        for g in range(4):
            cols = slice(256 * g, 256 * g + 256)
            scores = jnp.dot(keys, qt[:, cols], preferred_element_type=F32)
            scores = jnp.where(allowed, scores, -1e30)
            old = run_max[g, 0:1, :]
            new = jnp.maximum(old, jnp.max(scores, axis=0, keepdims=True))
            expo = jnp.exp2(scores - new)
            decay = jnp.exp2(old - new)
            run_max[g, 0:1, :] = new
            run_sum[g, 0:1, :] = run_sum[g, 0:1, :] * decay + jnp.sum(expo, axis=0, keepdims=True)
            grad_dots = jnp.dot(values, dot_[:, cols], preferred_element_type=F32)
            weighted = (expo * grad_dots).astype(BF16)
            acc[:, cols] = acc[:, cols] * decay + jnp.dot(kvt, expo.astype(BF16), preferred_element_type=F32)
            acc2[:, cols] = acc2[:, cols] * decay + jnp.dot(kvt[:128], weighted, preferred_element_type=F32)
        return carry

    lax.fori_loop(first, chip + 1, chunk, 0)

    cosine, sine = cos_ref[...], sin_ref[...]
    for g in range(4):
        cols = slice(256 * g, 256 * g + 256)
        lanes = slice(128 * g, 128 * g + 128)
        inverse = 1.0 / run_sum[g, 0:1, :]
        out = acc[128:256, cols] * inverse
        mean_dot = jnp.sum(dot_[:, cols].astype(F32) * out, axis=0, keepdims=True)
        grad = (acc2[:, cols] - mean_dot * acc[0:128, cols]) * (inverse * SOFT_SCALE)
        ga, gb = grad[:64], grad[64:]
        back = jnp.concatenate([ga * cosine + gb * sine, gb * cosine - ga * sine], axis=0)
        for b in range(2):
            ox_ref[b, :, lanes] = out[:, 128 * b : 128 * b + 128].T.astype(BF16)
            glx_ref[b, :, lanes] = back[:, 128 * b : 128 * b + 128].T.astype(BF16)


def attend(qx, dox, kvg, idg, cosine, sine):
    vmem = pl.BlockSpec(memory_space=pltpu.VMEM)
    return pl.pallas_call(
        attend_kernel,
        name="attend",
        out_shape=(jax.ShapeDtypeStruct((2, 128, 512), BF16), jax.ShapeDtypeStruct((2, 128, 512), BF16)),
        in_specs=[vmem] * 6,
        out_specs=(vmem, vmem),
        scratch_shapes=[
            pltpu.VMEM((128, 1024), BF16),
            pltpu.VMEM((128, 1024), BF16),
            pltpu.VMEM((4, 8, 256), F32),
            pltpu.VMEM((4, 8, 256), F32),
            pltpu.VMEM((256, 1024), F32),
            pltpu.VMEM((128, 1024), F32),
        ],
        compiler_params=pltpu.CompilerParams(vmem_limit_bytes=VMEM_LIMIT),
    )(qx, dox, kvg, idg, cosine, sine)


def reduce_kernel(
    ox_ref, glx_ref, lowx_ref, normed_ref, up_ref,
    attn_ref, grad_at_ref, up_out_ref,
    mid_send, mid_recv, buf, rcore, b1, rx, b2, ry, b3, rz, final,
    p_send, p_recv, x_send, x_recv, y_send, y_recv, z_send, z_recv,
    gy_send, gy_recv, gx_send, gx_recv,
):
    x, y, z, j, f = places()
    i = 1 - j
    sibling = ctx_of(x, y, z, i)
    xs = [(x + d) % 4 for d in (1, 2, 3)]
    ys = [(y + d) % 4 for d in (1, 2, 3)]
    whole_z = f * 4 + z
    zs = [(whole_z + d) % 8 for d in range(1, 8)]

    barrier = pltpu.get_barrier_semaphore()
    peers = [(sibling, f)]
    peers += [(ctx_of(p, y, z, j), f) for p in xs]
    peers += [(ctx_of(x, p, z, j), f) for p in ys]
    peers += [(ctx_of(x, y, p % 4, j), p // 4) for p in zs]
    for peer in peers:
        pl.semaphore_signal(barrier, inc=1, device_id=peer, device_id_type=MESH)

    glx = jnp.concatenate([glx_ref[0], glx_ref[1]], axis=0)
    up = up_ref[:, pl.ds(pl.multiple_of(512 * j, 512), 512)]
    midt = ADAPTER_SCALE * lax.dot_general(
        up, glx, (((1,), (1,)), ((), ())), preferred_element_type=F32
    )
    mid_send[0] = midt[:, 0:128]
    mid_send[1] = midt[:, 128:256]
    pl.semaphore_wait(barrier, len(peers))

    sent = []
    mid_copy = remote(mid_send.at[i], mid_recv, p_send.at[0], p_recv.at[0], sibling, f)
    mid_copy.start()
    near = pl.ds(pl.multiple_of(512 * j, 512), 512)
    out_copy = remote(ox_ref.at[i], attn_ref.at[:, near], p_send.at[1], p_recv.at[1], sibling, f)
    out_copy.start()
    attn_ref[:, near] = ox_ref[j]

    lowt = jnp.concatenate([lowx_ref[0], lowx_ref[1]], axis=1)
    upg = ADAPTER_SCALE * jnp.dot(lowt, glx, preferred_element_type=F32)
    buf[64:96] = jnp.zeros((32, 8, 128), F32)
    for s in range(2):
        for t in range(4):
            buf[64 + 16 * s + 8 * f + 4 * j + t] = upg[8 * s : 8 * s + 8, 128 * t : 128 * t + 128]
    mid_copy.wait()
    mid = (mid_send[j] + mid_recv[...]).astype(BF16)
    for t in range(4):
        part = jnp.dot(mid, normed_ref[:, 1024 * t : 1024 * t + 1024], preferred_element_type=F32)
        for s in range(2):
            for w in range(8):
                buf[32 * s + 8 * t + w] = part[8 * s : 8 * s + 8, 128 * w : 128 * w + 128]

    core_copy = remote(buf.at[pl.ds(48 * i, 48)], rcore, p_send.at[2], p_recv.at[2], sibling, f)
    core_copy.start()
    core_copy.wait()
    b1[...] = buf[pl.ds(48 * j, 48)] + rcore[...]
    copies = []
    for n, p in enumerate(xs):
        copy = remote(b1.at[pl.ds(12 * p, 12)], rx.at[n], x_send.at[n], x_recv.at[n], ctx_of(p, y, z, j), f)
        copy.start()
        copies.append(copy)
    for copy in copies:
        copy.wait()
    b2[...] = b1[pl.ds(12 * x, 12)] + rx[0] + rx[1] + rx[2]
    copies = []
    for n, p in enumerate(ys):
        copy = remote(b2.at[pl.ds(3 * p, 3)], ry.at[n], y_send.at[n], y_recv.at[n], ctx_of(x, p, z, j), f)
        copy.start()
        copies.append(copy)
    for copy in copies:
        copy.wait()
    b3[...] = b2[pl.ds(3 * y, 3)] + ry[0] + ry[1] + ry[2]
    copies = []
    for n, p in enumerate(zs):
        copy = remote(b3, rz.at[whole_z], z_send.at[n], z_recv.at[n], ctx_of(x, y, p % 4, j), p // 4)
        copy.start()
        copies.append(copy)
    rz[whole_z] = b3[...]
    for n, copy in enumerate(copies):
        source = (whole_z + 7 - n) % 8
        remote(rz.at[source], rz.at[source], z_send.at[n], z_recv.at[n], sibling, f).wait_recv()
    added = rz[0]
    for n in range(1, 8):
        added = added + rz[n]
    row = 48 * j + 12 * x + 3 * y
    final[pl.ds(row, 3)] = added
    sent += copies

    for n, p in enumerate(ys):
        part = final.at[pl.ds(row, 3)]
        copy = remote(part, part, gy_send.at[n], gy_recv.at[n], ctx_of(x, p, z, j), f)
        copy.start()
        sent.append(copy)
    for n in range(3):
        part = final.at[pl.ds(48 * j + 12 * x + 3 * ((y + 3 - n) % 4), 3)]
        remote(part, part, gy_send.at[n], gy_recv.at[n], sibling, f).wait_recv()
    for n, p in enumerate(xs):
        part = final.at[pl.ds(48 * j + 12 * x, 12)]
        copy = remote(part, part, gx_send.at[n], gx_recv.at[n], ctx_of(p, y, z, j), f)
        copy.start()
        sent.append(copy)
    for n in range(3):
        part = final.at[pl.ds(48 * j + 12 * ((x + 3 - n) % 4), 12)]
        remote(part, part, gx_send.at[n], gx_recv.at[n], sibling, f).wait_recv()
    part = final.at[pl.ds(48 * j, 48)]
    copy = remote(part, part, p_send.at[3], p_recv.at[3], sibling, f)
    copy.start()
    sent.append(copy)
    part = final.at[pl.ds(48 * i, 48)]
    remote(part, part, p_send.at[3], p_recv.at[3], sibling, f).wait_recv()

    for s in range(2):
        for t in range(32):
            grad_at_ref[8 * s : 8 * s + 8, 128 * t : 128 * t + 128] = final[32 * s + t]
        for t in range(8):
            up_out_ref[8 * s : 8 * s + 8, 128 * t : 128 * t + 128] = final[64 + 16 * s + 8 * f + t]

    other_half = attn_ref.at[:, pl.ds(pl.multiple_of(512 * i, 512), 512)]
    remote(ox_ref.at[i], other_half, p_send.at[1], p_recv.at[1], sibling, f).wait_recv()
    out_copy.wait_send()
    for copy in sent:
        copy.wait_send()


def reduce_all(ox, glx, lowx, normed, up):
    vmem = pl.BlockSpec(memory_space=pltpu.VMEM)
    hbm = pl.BlockSpec(memory_space=pl.ANY)
    dma = pltpu.SemaphoreType.DMA
    tiles = lambda *lead: pltpu.VMEM((*lead, 8, 128), F32)
    return pl.pallas_call(
        reduce_kernel,
        name="reduce_all",
        out_shape=(
            jax.ShapeDtypeStruct((128, 1024), BF16),
            jax.ShapeDtypeStruct((16, 4096), F32),
            jax.ShapeDtypeStruct((16, 1024), F32),
        ),
        in_specs=[vmem] * 5,
        out_specs=(vmem, vmem, vmem),
        scratch_shapes=[
            pltpu.VMEM((2, 16, 128), F32),
            pltpu.VMEM((16, 128), F32),
            tiles(96), tiles(48), tiles(48), tiles(3, 12), tiles(12), tiles(3, 3), tiles(3), tiles(8, 3),
            tiles(96),
        ]
        + [dma((n,)) for n in (4, 4, 3, 3, 3, 3, 7, 7, 3, 3, 3, 3)],
        compiler_params=pltpu.CompilerParams(
            collective_id=2, has_side_effects=True, vmem_limit_bytes=VMEM_LIMIT
        ),
    )(ox, glx, lowx, normed, up)


def on_device(
    layer_input,
    gain,
    codes,
    column_scale_quantized,
    block_second_scale,
    query_down_map,
    query_up_map,
    token_document,
    output_cotangent,
):
    place = lax.axis_index("ctx")
    chip = place // 2
    freqs = jnp.exp(jnp.arange(HEAD // 2, dtype=F32) * (-2.0 * math.log(ROPE_BASE) / HEAD))
    chip_positions = (chip * 256 + jnp.arange(256, dtype=I32)).astype(F32)
    angle_t = freqs[:, None] * chip_positions[None, :]
    cos_t, sin_t = jnp.cos(angle_t), jnp.sin(angle_t)
    cosine = lax.dynamic_slice_in_dim(cos_t, (place % 2) * 128, 128, 1).T
    sine = lax.dynamic_slice_in_dim(sin_t, (place % 2) * 128, 128, 1).T
    cosine = jnp.concatenate([cosine, cosine], axis=1)
    sine = jnp.concatenate([-sine, sine], axis=1)
    table = jnp.asarray(NF4_LEVELS * 8, F32)[None, :]
    ids = jnp.broadcast_to(token_document[None, :], (8, 128))

    q, kv, normed, lowt = project(
        layer_input,
        gain[None, :],
        codes,
        column_scale_quantized,
        block_second_scale[:, None],
        query_down_map.T,
        query_up_map,
        cosine,
        sine,
        table,
    )
    qx, dox, kvg, idg, lowx = gather(q, kv, output_cotangent, lowt, ids)
    ox, glx = attend(qx, dox, kvg, idg, cos_t, sin_t)
    attn, grad_at, up_map_gradient = reduce_all(ox, glx, lowx, normed, query_up_map)
    return (attn, grad_at.T, up_map_gradient)


def solution(mesh):
    return jax.shard_map(
        on_device,
        mesh=mesh,
        in_specs=(
            P("ctx", None),
            P(),
            P("fsdp", None),
            P("fsdp", None),
            P(),
            P(),
            P(None, "fsdp"),
            P("ctx"),
            P("ctx", "fsdp"),
        ),
        out_specs=(P("ctx", "fsdp"), P(), P(None, "fsdp")),
        check_vma=False,
    )
```

time: 1300 us -> 222 us (0.17)
  waiting for transfers between devices: 777 us -> 0 us
  blocking collectives: 219 us -> 0 us
  Pallas kernels: 0 us -> 212 us
  local copies, waits for them, and re-layouts: 165 us -> 8.9 us
  other arithmetic: 58.3 us -> 0.34 us
  matrix products: 39.3 us -> 0 us
  between operations: 14.4 us -> 0.75 us
  starting transfers between devices: 13.1 us -> 0 us
    all_gather x2 -> x0, waiting for transfers between devices: 518 us -> none  [the longest x1 496 us: total_of_pieces(): return lax.all_gather(array, axis).sum(0)]
    psum x1 -> x0, waiting for transfers between devices: 252 us -> none  [on_device(): grad_a = lax.psum(local_a, ('ctx', 'fsdp'))]
    all_gather x1 -> x0, blocking collectives: 219 us -> none  [on_device(): all_ids = lax.all_gather(token_document, 'ctx', axis=0, tiled=True)]
    pallas_call x0 -> x4, Pallas kernels: none -> 212 us  [the longest x1 96.5 us: reduce_all(): pl.pallas_call(reduce_kernel, name='reduce_all', out_shape=(jax.ShapeDtyp...]
    and x16 -> x0, local copies, waits for them, and re-layouts: 84.5 us -> none  [dequantize(): jnp.bitwise_and(jnp.right_shift(packed, 4 * nibble), 15)]
    add x6 -> x0, other arithmetic: 39.7 us -> none  [the longest x1 38.7 us: dequantize(): levels + jnp.where(unpacked == slot_code, jnp.float32(level_value), jnp.f...]
    dot_general x10 -> x0, matrix products: 39.3 us -> none  [the longest x1 27.1 us: on_device(): jnp.dot(input_normalized, weight, preferred_element_type=jnp.float32)]
    mul x2 -> x0, local copies, waits for them, and re-layouts: 37.8 us -> none  [dequantize(): scaled = levels.reshape(row_count // 64, 64, -1) * absmax[:, None, :]]
  transfers between devices with their start and end apart: 5 -> 0, of which waited for: 4 -> 0; matrix products, arithmetic and copies ran while one was open for 4% -> 0% of each run, Pallas kernels for 0% -> 0%
where the time goes in v1:
time: 222 us
  Pallas kernels  212 us (95%)
  local copies, waits for them, and re-layouts  8.9 us (4%)
    pallas_call x1, Pallas kernels, reduce_all(): pl.pallas_call(reduce_kernel, name='reduce_all', out_shape=(jax.ShapeDtyp...  96.5 us
    pallas_call x1, Pallas kernels, gather(): pl.pallas_call(gather_kernel, name='gather', out_shape=(jax.ShapeDtypeStr...  67.3 us
    pallas_call x1, Pallas kernels, project(): pl.pallas_call(project_kernel, name='project', out_shape=(jax.ShapeDtypeS...  41.3 us
    pallas_call x1, Pallas kernels, attend(): pl.pallas_call(attend_kernel, name='attend', out_shape=(jax.ShapeDtypeStr...  6.84 us
    unnamed x7, local copies, waits for them, and re-layouts  4.82 us

profile of v1, /device:TPU:1, one launch (start us, length us, event | category | flops | bytes accessed | tf_op | source)
XLA Modules:
  0.0 221.9 jit_solution(16732892178468006687)
XLA Ops:
  0.7 1.2 broadcast_in_dim.20.ids_ref
  1.9 1.4 copy.13.bs_ref
  3.3 0.3 multiply_sine_fusion
  3.6 0.0 copy-start
  3.6 0.0 copy-start.1
  3.6 0.7 copy.14.cos_ref
  4.4 0.7 copy.15.sin_ref
  5.1 41.3 %project.1 = (bf16[128,1024]{1,0:T(8,128)(2,1)}, bf16[2,128,256]{2,1,0:T(8,128)(2,1)}, bf16[128,4096]{1,0:T(8,128)(2,1)}, bf16[16,128]{1,0:T(8,128)(2,1)}) custom-call(bf16[128,4096]{1,0:T(8,128)(2,1)} %x_ref.1, f32[1,4096]{1,0:T(1,128)} %bitcast.11, s32[2048,384]{1,0:T(8,128)} %codes_ref.1, s32[32,3072]{1,0:T(8,128)} %sq_ref.1, f32[64,1]{1,0:T(8,128)} %copy.13.bs_ref, ...), custom_call_target="tpu_custom_call" | custom-call | tf_op jit(solution)/shard_map/project/pallas_call | solution.py:169
  46.4 67.3 %gather.1 = (bf16[2,128,512]{2,1,0:T(8,128)(2,1)}, bf16[2,128,512]{2,1,0:T(8,128)(2,1)}, bf16[64,2,128,256]{3,2,1,0:T(8,128)(2,1)}, s32[64,2,8,128]{3,2,1,0:T(8,128)}, bf16[2,16,128]{2,1,0:T(8,128)(2,1)}) custom-call(bf16[128,1024]{1,0:T(8,128)(2,1)} %get-tuple-element.17.q_ref, bf16[2,128,256]{2,1,0:T(8,128)(2,1)} %get-tuple-element.18.kv_ref, ...), custom_call_target="tpu_custom_call" | custom-call | tf_op jit(solution)/shard_map/gather/pallas_call | solution.py:362
  113.7 0.0 copy-done
  113.7 0.0 copy-done.1
  113.7 6.8 %attend.1 = (bf16[2,128,512]{2,1,0:T(8,128)(2,1)}, bf16[2,128,512]{2,1,0:T(8,128)(2,1)}) custom-call(bf16[2,128,512]{2,1,0:T(8,128)(2,1)} %get-tuple-element.20.qx_ref, bf16[2,128,512]{2,1,0:T(8,128)(2,1)} %get-tuple-element.21.dox_ref, bf16[64,2,128,256]{3,2,1,0:T(8,128)(2,1)} %get-tuple-element.22.kvg_ref, s32[64,2,8,128]{3,2,1,0:T(8,128)} %get-tuple-element.23.idg_ref, ...), custom_call_target="tpu_custom_call" | custom-call | tf_op jit(solution)/shard_map/attend/pallas_call | solution.py:454
  120.6 96.5 %reduce_all.1 = (bf16[128,1024]{1,0:T(8,128)(2,1)}, f32[16,4096]{1,0:T(8,128)}, f32[16,1024]{1,0:T(8,128)}) custom-call(bf16[2,128,512]{2,1,0:T(8,128)(2,1)} %get-tuple-element.24.ox_ref, bf16[2,128,512]{2,1,0:T(8,128)(2,1)} %get-tuple-element.25.glx_ref, bf16[2,16,128]{2,1,0:T(8,128)(2,1)} %get-tuple-element.26.lowx_ref, ...), custom_call_target="tpu_custom_call" | custom-call | tf_op jit(solution)/shard_map/reduce_all/pallas_call | solution.py:603
  217.1 1.7 copy.19
  218.7 1.7 copy.20
  220.4 1.5 copy.21
  (6 shorter events, 0.0 us)
Async XLA Ops:
  3.6 110.1 %copy-start = (f32[64,256]{1,0:T(8,128)}, f32[64,256]{1,0:T(8,128)S(1)}, u32[]{:S(2)}) copy-start(f32[64,256]{1,0:T(8,128)S(1)} %get-tuple-element.33.sin_ref) | copy-start | bytes 196612
  3.6 110.1 %copy-start.1 = (f32[64,256]{1,0:T(8,128)}, f32[64,256]{1,0:T(8,128)S(1)}, u32[]{:S(2)}) copy-start(f32[64,256]{1,0:T(8,128)S(1)} %get-tuple-element.34.cos_ref) | copy-start | bytes 196612

commit v2 on v1

v2 whole, which is shorter than its diff:
```python
import functools
import math

import jax
import jax.numpy as jnp
from jax import lax
from jax.experimental import pallas as pl
from jax.experimental.pallas import tpu as pltpu
from jax.sharding import PartitionSpec as P

MESH = pl.DeviceIdType.MESH
HEAD = 128
NF4_LEVELS = [
    -1.0,
    -0.6961928009986877,
    -0.5250730514526367,
    -0.39491748809814453,
    -0.28444138169288635,
    -0.18477343022823334,
    -0.09105003625154495,
    0.0,
    0.07958029955625534,
    0.16093020141124725,
    0.24611230194568634,
    0.33791524171829224,
    0.44070982933044434,
    0.5626170039176941,
    0.7229568362236023,
    1.0,
]
ADAPTER_SCALE = 2.0
ROPE_BASE = 500000.0
SOFT_SCALE = 1.0 / math.sqrt(HEAD)
QUERY_SCALE = SOFT_SCALE * math.log2(math.e)
F32, BF16, I32 = jnp.float32, jnp.bfloat16, jnp.int32
VMEM_LIMIT = 60 * 1024 * 1024


def places():
    c = lax.axis_index("ctx")
    f = lax.axis_index("fsdp")
    return c // 32, (c // 8) % 4, (c // 2) % 4, c % 2, f


def ctx_of(x, y, z, j):
    return ((x * 4 + y) * 4 + z) * 2 + j


def pair_of(x, y, z, j):
    return ctx_of(3 - x, 3 - y, (z + 2) % 4, j)


def lookup(table, index):
    return lax.gather(
        table,
        index[..., None],
        lax.GatherDimensionNumbers(
            offset_dims=(),
            collapsed_slice_dims=(1,),
            start_index_map=(1,),
            operand_batching_dims=(0,),
            start_indices_batching_dims=(0,),
        ),
        slice_sizes=(1, 1),
        mode=lax.GatherScatterMode.PROMISE_IN_BOUNDS,
    )


def remote(src, dst, send, recv, ctx, f):
    return pltpu.make_async_remote_copy(
        src_ref=src, dst_ref=dst, send_sem=send, recv_sem=recv, device_id=(ctx, f), device_id_type=MESH
    )


def project_kernel(
    x_ref, gain_ref, codes_ref, sq_ref, bs_ref, downt_ref, up_ref, cos_ref, sin_ref, table_ref, doc_ref, do_ref,
    q_ref, kv_ref, normed_ref, lowt_ref, ids_ref, dox,
    perm, scale, w_buf, acc, nat, send_main, send_half, recv_main, recv_half, total, send_sem, recv_sem,
):
    x, y, z, j, f = places()
    c = lax.axis_index("ctx")
    other = 1 - f
    pair = pair_of(x, y, z, j)
    k = z // 2
    barrier = pltpu.get_barrier_semaphore()
    pl.semaphore_signal(barrier, inc=1, device_id=(c, other), device_id_type=MESH)
    pl.semaphore_signal(barrier, inc=1, device_id=(pair, f), device_id_type=MESH)

    wide = x_ref[...].astype(F32)
    inverse = lax.rsqrt(jnp.mean(wide * wide, axis=-1, keepdims=True) + 1e-05)
    normed_ref[...] = (wide * inverse * gain_ref[...]).astype(BF16)
    ids_ref[...] = jnp.broadcast_to(doc_ref[...], (8, 128))
    dox[0] = do_ref[:, pl.ds(pl.multiple_of(512 * k, 512), 512)]

    pl.semaphore_wait(barrier, 2)
    far = pl.ds(pl.multiple_of(512 * (1 - k), 512), 512)
    copy_do = remote(do_ref.at[:, far], dox.at[1], send_sem.at[2], recv_sem.at[2], pair, f)
    copy_do.start()

    for part in range(8):
        m = lax.broadcasted_iota(I32, (128, 1024), 0)
        k = lax.broadcasted_iota(I32, (128, 1024), 1)
        perm[128 * part : 128 * part + 128, :] = jnp.where(k == 8 * m + part, 1.0, 0.0).astype(BF16)
    pick = lax.broadcasted_iota(I32, (32, 64), 1) == lax.broadcasted_iota(I32, (32, 64), 0) + 32 * f
    second = jnp.sum(jnp.where(pick, bs_ref[...], 0.0), axis=1, keepdims=True) * (1.0 / 256.0)
    for t in range(3):
        quantized = (sq_ref[:, 1024 * t : 1024 * t + 1024].astype(F32) + 1.0).astype(BF16)
        packed = lax.dot_general(quantized, perm[...], (((1,), (1,)), ((), ())), preferred_element_type=F32)
        scale[t] = packed * second

    table = jnp.broadcast_to(table_ref[...], (64, 128))

    def tile(t):
        lane = pl.multiple_of(t * 128, 128)
        acc[...] = jnp.zeros_like(acc)

        def chunk(kc, carry):
            for b in range(4):
                row = pl.multiple_of(kc * 256 + b * 64, 64)
                words = codes_ref[pl.ds(row, 64), pl.ds(lane, 128)]
                scale_row = scale[t, pl.ds(kc * 4 + b, 1), :]
                for n in range(8):
                    index = jnp.bitwise_and(jnp.right_shift(words, 4 * n), 15)
                    levels = lookup(table, index)
                    w_buf[64 * b : 64 * b + 64, 128 * n : 128 * n + 128] = (
                        levels * scale_row[:, 128 * n : 128 * n + 128]
                    ).astype(BF16)
            col = pl.multiple_of(f * 2048 + kc * 256, 256)
            acc[...] += jnp.dot(normed_ref[:, pl.ds(col, 256)], w_buf[...], preferred_element_type=F32)
            return carry

        lax.fori_loop(0, 8, chunk, 0)
        full = acc[...]
        high = full.astype(BF16)
        low = (full - high.astype(F32)).astype(BF16)
        nat[...] = jnp.dot(high, perm[...], preferred_element_type=F32) + jnp.dot(
            low, perm[...], preferred_element_type=F32
        )

    own_main = pl.ds(pl.multiple_of(512 * f, 512), 1024)
    own_half = pl.ds(pl.multiple_of(1024 * (1 - f), 512), 512)

    tile(2 * (1 - f))
    send_main[...] = nat[...].astype(BF16)
    copy_main = remote(send_main, recv_main, send_sem.at[0], recv_sem.at[0], c, other)
    copy_main.start()
    tile(1)
    send_half[...] = nat[:, pl.ds(pl.multiple_of(512 * (1 - f), 512), 512)].astype(BF16)
    copy_half = remote(send_half, recv_half, send_sem.at[1], recv_sem.at[1], c, other)
    copy_half.start()
    total[:, own_half] = nat[:, pl.ds(pl.multiple_of(512 * f, 512), 512)]
    tile(2 * f)
    total[:, own_main] = nat[...]

    lowt = lax.dot_general(
        downt_ref[...], normed_ref[...], (((1,), (1,)), ((), ())), preferred_element_type=F32
    ).astype(BF16)
    lowt_ref[...] = lowt
    nat[...] = ADAPTER_SCALE * lax.dot_general(
        lowt, up_ref[...], (((0,), (0,)), ((), ())), preferred_element_type=F32
    )

    copy_main.wait()
    total[:, own_main] += recv_main[...].astype(F32)
    copy_half.wait()
    total[:, own_half] += recv_half[...].astype(F32)

    cosine, sine = cos_ref[0].T, sin_ref[0].T
    cosine = jnp.concatenate([cosine, cosine], axis=1)
    sine = jnp.concatenate([-sine, sine], axis=1)

    def rotate(v):
        return v * cosine + pltpu.roll(v, 64, 1) * sine

    for h in range(8):
        s = slice(128 * h, 128 * h + 128)
        q_ref[:, s] = (rotate(total[:, s] + nat[:, s]) * QUERY_SCALE).astype(BF16)
    for h in range(2):
        kv_ref[h, :, 0:128] = rotate(total[:, 1024 + 128 * h : 1152 + 128 * h]).astype(BF16)
        kv_ref[h, :, 128:256] = total[:, 1280 + 128 * h : 1408 + 128 * h].astype(BF16)
    copy_do.wait()


def project(x, gain, codes, sq, bs, downt, up, cosine, sine, table, doc, do):
    vmem = pl.BlockSpec(memory_space=pltpu.VMEM)
    return pl.pallas_call(
        project_kernel,
        name="project",
        out_shape=(
            jax.ShapeDtypeStruct((128, 1024), BF16),
            jax.ShapeDtypeStruct((2, 128, 256), BF16),
            jax.ShapeDtypeStruct((128, 4096), BF16),
            jax.ShapeDtypeStruct((16, 128), BF16),
            jax.ShapeDtypeStruct((8, 128), I32),
            jax.ShapeDtypeStruct((2, 128, 512), BF16),
        ),
        in_specs=[vmem] * 12,
        out_specs=(vmem,) * 6,
        scratch_shapes=[
            pltpu.VMEM((1024, 1024), BF16),
            pltpu.VMEM((3, 32, 1024), F32),
            pltpu.VMEM((256, 1024), BF16),
            pltpu.VMEM((128, 1024), F32),
            pltpu.VMEM((128, 1024), F32),
            pltpu.VMEM((128, 1024), BF16),
            pltpu.VMEM((128, 512), BF16),
            pltpu.VMEM((128, 1024), BF16),
            pltpu.VMEM((128, 512), BF16),
            pltpu.VMEM((128, 1536), F32),
            pltpu.SemaphoreType.DMA((3,)),
            pltpu.SemaphoreType.DMA((3,)),
        ],
        compiler_params=pltpu.CompilerParams(
            collective_id=0, has_side_effects=True, vmem_limit_bytes=VMEM_LIMIT
        ),
    )(x, gain, codes, sq, bs, downt, up, cosine, sine, table, doc, do)


def gather_kernel(
    q_ref, kv_ref, lowt_ref, ids_ref,
    qx, kvg, idg, lowx,
    e_send, e_recv, own_sem, z_send, z_recv, zi_send, zi_recv, a_send, a_recv, ai_send, ai_recv,
    b_send, b_recv, bi_send, bi_recv, s_send, s_recv,
):
    x, y, z, j, f = places()
    i = 1 - j
    k = z // 2
    u = x * i + y * j
    v = y * i + x * j

    def at(uu, vv, zz):
        return ctx_of(uu * i + vv * j, vv * i + uu * j, zz, j)

    def slot(uu, vv, zz):
        return (uu * 4 + vv) * 4 + zz

    sibling = ctx_of(x, y, z, i)
    pair = pair_of(x, y, z, j)
    zo = (z + 2) % 4
    zn = z + 1 - 2 * (z % 2)
    zf = (zn + 2) % 4
    across, next_z, far_z = at(u, v, zo), at(u, v, zn), at(u, v, zf)
    vr, vl, vo = (v + 1) % 4, (v + 3) % 4, (v + 2) % 4
    ur, ul, uo = (u + 1) % 4, (u + 3) % 4, (u + 2) % 4
    right_v, left_v = at(u, vr, z), at(u, vl, z)
    right_u, left_u = at(ur, v, z), at(ul, v, z)

    barrier = pltpu.get_barrier_semaphore()
    peers = [sibling, pair, across, next_z, far_z, right_v, left_v, right_u, left_u]
    for peer in peers:
        pl.semaphore_signal(barrier, inc=1, device_id=(peer, f), device_id_type=MESH)
    pl.semaphore_wait(barrier, len(peers))

    sent = []

    def push(src, dst, n, send, recv, peer):
        copy = remote(src, dst, send.at[n], recv.at[n], peer, f)
        copy.start()
        sent.append(copy)

    def got(ref, n, send, recv):
        remote(ref, ref, send.at[n], recv.at[n], sibling, f).wait_recv()

    mine = slot(u, v, z)
    near = pl.ds(pl.multiple_of(512 * k, 512), 512)
    far = pl.ds(pl.multiple_of(512 * (1 - k), 512), 512)
    push(kv_ref.at[1 - k], kvg.at[j, mine], 0, e_send, e_recv, across)
    push(kv_ref.at[k], kvg.at[j, mine], 0, z_send, z_recv, next_z)
    for n, peer in enumerate((next_z, across, far_z)):
        push(ids_ref, idg.at[j, mine], n, zi_send, zi_recv, peer)
    push(q_ref.at[:, far], qx.at[1], 1, e_send, e_recv, pair)
    push(lowt_ref, lowx.at[1], 2, e_send, e_recv, pair)
    local = []
    for n, (src, dst) in enumerate(
        (
            (kv_ref.at[k], kvg.at[j, mine]),
            (ids_ref, idg.at[j, mine]),
            (q_ref.at[:, near], qx.at[0]),
            (lowt_ref, lowx.at[0]),
        )
    ):
        copy = pltpu.make_async_copy(src, dst, own_sem.at[n])
        copy.start()
        local.append(copy)

    second = kvg.at[j, slot(u, v, zo)]
    got(second, 0, e_send, e_recv)
    push(second, second, 1, z_send, z_recv, next_z)
    got(kvg.at[j, slot(u, v, zn)], 0, z_send, z_recv)
    for n, zz in enumerate((zn, zo, zf)):
        got(idg.at[j, slot(u, v, zz)], n, zi_send, zi_recv)
    local[0].wait()
    local[1].wait()
    got(kvg.at[j, slot(u, v, zf)], 1, z_send, z_recv)

    def half(vv, h):
        return kvg.at[j, pl.ds(slot(u, vv, 0) + 2 * h, 2)]

    def piece(uu, vv):
        return kvg.at[j, pl.ds(slot(uu, vv, 0), 4)]

    def marks(vv):
        return idg.at[j, pl.ds(slot(u, vv, 0), 4)]

    def all_marks(uu):
        return idg.at[j, pl.ds(slot(uu, 0, 0), 16)]

    def same(part, n, send, recv, peer):
        push(part, part, n, send, recv, peer)

    shared = []

    def share(du, dv):
        part = piece((u + du) % 4, (v + dv) % 4)
        same(part, len(shared), s_send, s_recv, sibling)
        shared.append((du, dv))

    same(half(v, 0), 0, a_send, a_recv, right_v)
    same(half(v, 1), 3, a_send, a_recv, left_v)
    same(half(v, 1), 1, a_send, a_recv, right_v)
    same(half(v, 0), 4, a_send, a_recv, left_v)
    same(marks(v), 0, ai_send, ai_recv, right_v)
    same(marks(v), 1, ai_send, ai_recv, left_v)
    same(piece(u, v), 0, b_send, b_recv, right_u)
    same(piece(u, v), 4, b_send, b_recv, left_u)
    share(0, 0)
    got(half(vl, 0), 0, a_send, a_recv)
    same(half(vl, 0), 2, a_send, a_recv, right_v)
    got(half(vr, 1), 3, a_send, a_recv)
    same(half(vr, 1), 5, a_send, a_recv, left_v)
    got(half(vl, 1), 1, a_send, a_recv)
    got(marks(vl), 0, ai_send, ai_recv)
    same(marks(vl), 2, ai_send, ai_recv, right_v)
    same(piece(u, vl), 1, b_send, b_recv, right_u)
    same(piece(u, vl), 5, b_send, b_recv, left_u)
    share(0, 3)
    got(half(vr, 0), 4, a_send, a_recv)
    got(marks(vr), 1, ai_send, ai_recv)
    same(piece(u, vr), 2, b_send, b_recv, right_u)
    same(piece(u, vr), 6, b_send, b_recv, left_u)
    share(0, 1)
    got(half(vo, 0), 2, a_send, a_recv)
    got(half(vo, 1), 5, a_send, a_recv)
    got(marks(vo), 2, ai_send, ai_recv)
    same(piece(u, vo), 3, b_send, b_recv, right_u)
    same(piece(u, vo), 7, b_send, b_recv, left_u)
    share(0, 2)
    same(all_marks(u), 0, bi_send, bi_recv, right_u)
    same(all_marks(u), 1, bi_send, bi_recv, left_u)

    got(piece(ul, v), 0, b_send, b_recv)
    same(piece(ul, v), 8, b_send, b_recv, right_u)
    share(3, 0)
    got(piece(ul, vl), 1, b_send, b_recv)
    same(piece(ul, vl), 9, b_send, b_recv, right_u)
    share(3, 3)
    got(piece(ur, vr), 6, b_send, b_recv)
    same(piece(ur, vr), 10, b_send, b_recv, left_u)
    share(1, 1)
    got(piece(ur, vo), 7, b_send, b_recv)
    same(piece(ur, vo), 11, b_send, b_recv, left_u)
    share(1, 2)
    got(all_marks(ul), 0, bi_send, bi_recv)
    same(all_marks(ul), 2, bi_send, bi_recv, right_u)
    got(all_marks(ur), 1, bi_send, bi_recv)
    got(piece(ul, vr), 2, b_send, b_recv)
    share(3, 1)
    got(piece(ul, vo), 3, b_send, b_recv)
    share(3, 2)
    got(piece(ur, v), 4, b_send, b_recv)
    share(1, 0)
    got(piece(ur, vl), 5, b_send, b_recv)
    share(1, 3)
    got(all_marks(uo), 2, bi_send, bi_recv)
    same(idg.at[j], 16, s_send, s_recv, sibling)
    got(piece(uo, v), 8, b_send, b_recv)
    share(2, 0)
    got(piece(uo, vr), 10, b_send, b_recv)
    share(2, 1)
    got(piece(uo, vl), 9, b_send, b_recv)
    share(2, 3)
    got(piece(uo, vo), 11, b_send, b_recv)
    share(2, 2)

    got(qx.at[1], 1, e_send, e_recv)
    got(lowx.at[1], 2, e_send, e_recv)
    for n, (du, dv) in enumerate(shared):
        got(kvg.at[i, pl.ds(slot((v + du) % 4, (u + dv) % 4, 0), 4)], n, s_send, s_recv)
    got(idg.at[i], 16, s_send, s_recv)
    for copy in local[2:]:
        copy.wait()
    for copy in sent:
        copy.wait_send()


def gather(q, kv, lowt, ids):
    vmem = pl.BlockSpec(memory_space=pltpu.VMEM)
    hbm = pl.BlockSpec(memory_space=pl.ANY)
    dma = pltpu.SemaphoreType.DMA
    counts = (3, 3, 4, 2, 2, 3, 3, 6, 6, 3, 3, 12, 12, 3, 3, 17, 17)
    return pl.pallas_call(
        gather_kernel,
        name="gather",
        out_shape=(
            jax.ShapeDtypeStruct((2, 128, 512), BF16),
            jax.ShapeDtypeStruct((2, 64, 128, 256), BF16),
            jax.ShapeDtypeStruct((2, 64, 8, 128), I32),
            jax.ShapeDtypeStruct((2, 16, 128), BF16),
        ),
        in_specs=[vmem] * 4,
        out_specs=(hbm,) * 4,
        scratch_shapes=[dma((n,)) for n in counts],
        compiler_params=pltpu.CompilerParams(
            collective_id=1, has_side_effects=True, vmem_limit_bytes=VMEM_LIMIT
        ),
    )(q, kv, lowt, ids)


STEP = 512


def attend_kernel(
    qx_ref, dox_ref, kvg_ref, idg_ref, cos_ref, sin_ref, ox_ref, glx_ref,
    qt, dot_, limits, ahead0, ahead1, max0, max1, run_max, run_sum, acc, acc2,
):
    x, y, z, j, _ = places()
    here = ctx_of(x, y, z, j)
    there = pair_of(x, y, z, j)

    def slot(number, core):
        a, b, d = number // 16, (number // 4) % 4, number % 4
        first, second = (a * 4 + b) * 4 + d, (b * 4 + a) * 4 + d
        if isinstance(core, int):
            return second if core else first
        return jnp.where(core == 0, first, second)

    def block(number):
        return jnp.concatenate([kvg_ref[0, slot(number, 0)], kvg_ref[1, slot(number, 1)]], axis=0)

    every = idg_ref[...].reshape(128, 8, 128)
    below = [
        jnp.sum(jnp.sum(jnp.where(every < d, 1, 0), axis=0), axis=1, keepdims=True)[0:1, :] for d in (1, 2, 3)
    ]
    lane = lax.broadcasted_iota(I32, (1, 128), 1)
    for t, place in enumerate((here, there)):
        ids = idg_ref[j, slot(place // 2, j), 0:1, :]
        start = jnp.zeros((1, 128), I32)
        for d in (1, 2, 3):
            start = jnp.where(ids == d, below[d - 1], start)
        limits[t, 0:1, :] = jnp.concatenate([start, start], axis=1)
        position = place * 128 + lane
        limits[t, 1:2, :] = jnp.concatenate([position, position], axis=1)
        for g in range(4):
            lanes = slice(128 * g, 128 * g + 128)
            qt[t, :, lanes] = qx_ref[t, :, lanes].T
            dot_[t, :, lanes] = dox_ref[t, :, lanes].T
    run_max[...] = jnp.full_like(run_max, -1e29)
    run_sum[...] = jnp.zeros_like(run_sum)
    acc[...] = jnp.zeros_like(acc)
    acc2[...] = jnp.zeros_like(acc2)

    def rows(t, carry):
        place = jnp.where(t == 0, here, there)
        first = jnp.min(limits[t, 0:1, :]) // STEP
        latest = jnp.max(limits[t, 0:1, :])
        stop = (place * 128 + 127) // STEP + 1

        def scores_of(number, masked, ahead, ahead_max):
            key = jnp.minimum(number, 31) * 2
            base = number * STEP
            for h in range(2):
                keys = block(key + h)[:, :128]
                for p in range(2):
                    cols = slice(256 * p, 256 * p + 256)
                    scores = jnp.dot(keys, qt[t, :, cols], preferred_element_type=F32)
                    if masked:
                        pos = base + 256 * h + lax.broadcasted_iota(I32, (256, 256), 0)
                        allowed = (pos >= limits[t, 0:1, :]) & (pos <= limits[t, 1:2, :])
                        scores = jnp.where(allowed, scores, -1e30)
                    ahead[256 * h : 256 * h + 256, cols] = scores
                    top = jnp.max(scores, axis=0, keepdims=True)
                    ahead_max[h : h + 1, cols] = top

        def is_edge(number):
            return (number * STEP < latest) | (number * STEP + STEP - 1 > place * 128)

        def step(number, masked, ahead, ahead_max, later, later_max):
            scores_of(number + 1, masked, later, later_max)
            kv = jnp.concatenate([block(2 * number), block(2 * number + 1)], axis=0)
            kvt = kv.T
            values = kv[:, 128:]
            for p in range(2):
                cols = slice(256 * p, 256 * p + 256)
                tops = jnp.maximum(ahead_max[0:1, cols], ahead_max[1:2, cols])
                old = run_max[t, 0:1, cols]
                new = jnp.maximum(old, tops)
                decay = jnp.exp2(old - new)
                run_max[t, 0:1, cols] = new
                grad_dots = jnp.dot(values, dot_[t, :, cols], preferred_element_type=F32)
                expo = jnp.exp2(ahead[:, cols] - new)
                run_sum[t, 0:1, cols] = run_sum[t, 0:1, cols] * decay + jnp.sum(expo, axis=0, keepdims=True)
                weighted = (expo * grad_dots).astype(BF16)
                acc[t, :, cols] = acc[t, :, cols] * decay + jnp.dot(
                    kvt, expo.astype(BF16), preferred_element_type=F32
                )
                acc2[t, :, cols] = acc2[t, :, cols] * decay + jnp.dot(
                    kvt[:128], weighted, preferred_element_type=F32
                )

        scores_of(first, True, ahead0, max0)

        def one(number, *buffers):
            edge = is_edge(number + 1)

            @pl.when(edge)
            def _():
                step(number, True, *buffers)

            @pl.when(jnp.logical_not(edge))
            def _():
                step(number, False, *buffers)

        def body(twice, c):
            number = first + 2 * twice
            one(number, ahead0, max0, ahead1, max1)

            @pl.when(number + 1 < stop)
            def _():
                one(number + 1, ahead1, max1, ahead0, max0)

            return c

        lax.fori_loop(0, (stop - first + 1) // 2, body, 0)
        return carry

    lax.fori_loop(0, 2, rows, 0)

    for t in range(2):
        cosine, sine = cos_ref[t], sin_ref[t]
        for g in range(4):
            lanes = slice(128 * g, 128 * g + 128)
            inverse = 1.0 / run_sum[t, 0:1, lanes]
            out = acc[t, 128:256, lanes] * inverse
            mean_dot = jnp.sum(dot_[t, :, lanes].astype(F32) * out, axis=0, keepdims=True)
            grad = (acc2[t, :, lanes] - mean_dot * acc[t, 0:128, lanes]) * (inverse * SOFT_SCALE)
            ga, gb = grad[:64], grad[64:]
            back = jnp.concatenate([ga * cosine + gb * sine, gb * cosine - ga * sine], axis=0)
            ox_ref[t, :, lanes] = out.T.astype(BF16)
            glx_ref[t, :, lanes] = back.T.astype(BF16)


def attend(qx, dox, kvg, idg, cosine, sine):
    vmem = pl.BlockSpec(memory_space=pltpu.VMEM)
    return pl.pallas_call(
        attend_kernel,
        name="attend",
        out_shape=(jax.ShapeDtypeStruct((2, 128, 512), BF16), jax.ShapeDtypeStruct((2, 128, 512), BF16)),
        in_specs=[vmem] * 6,
        out_specs=(vmem, vmem),
        scratch_shapes=[
            pltpu.VMEM((2, 128, 512), BF16),
            pltpu.VMEM((2, 128, 512), BF16),
            pltpu.VMEM((2, 8, 256), I32),
            pltpu.VMEM((512, 512), F32),
            pltpu.VMEM((512, 512), F32),
            pltpu.VMEM((8, 512), F32),
            pltpu.VMEM((8, 512), F32),
            pltpu.VMEM((2, 8, 512), F32),
            pltpu.VMEM((2, 8, 512), F32),
            pltpu.VMEM((2, 256, 512), F32),
            pltpu.VMEM((2, 128, 512), F32),
        ],
        compiler_params=pltpu.CompilerParams(vmem_limit_bytes=VMEM_LIMIT),
    )(qx, dox, kvg, idg, cosine, sine)


def reduce_kernel(
    ox_ref, glx_ref, lowx_ref, normed_ref, up_ref,
    attn_ref, grad_at_ref, up_out_ref,
    mid_send, mid_recv, buf, rcore, b1, rx, b2, ry, b3, rz, final,
    p_send, p_recv, x_send, x_recv, y_send, y_recv, z_send, z_recv,
    gy_send, gy_recv, gx_send, gx_recv,
):
    x, y, z, j, f = places()
    i = 1 - j
    sibling = ctx_of(x, y, z, i)
    xs = [(x + d) % 4 for d in (1, 2, 3)]
    ys = [(y + d) % 4 for d in (1, 2, 3)]
    whole_z = f * 4 + z
    zs = [(whole_z + d) % 8 for d in range(1, 8)]

    pair = pair_of(x, y, z, j)
    k = z // 2
    barrier = pltpu.get_barrier_semaphore()
    peers = [(sibling, f), (pair, f)]
    peers += [(ctx_of(p, y, z, j), f) for p in xs]
    peers += [(ctx_of(x, p, z, j), f) for p in ys]
    peers += [(ctx_of(x, y, p % 4, j), p // 4) for p in zs]
    for peer in peers:
        pl.semaphore_signal(barrier, inc=1, device_id=peer, device_id_type=MESH)

    glx = jnp.concatenate([glx_ref[0], glx_ref[1]], axis=0)
    up = up_ref[:, pl.ds(pl.multiple_of(512 * k, 512), 512)]
    midt = ADAPTER_SCALE * lax.dot_general(
        up, glx, (((1,), (1,)), ((), ())), preferred_element_type=F32
    )
    mid_send[0] = midt[:, 0:128]
    mid_send[1] = midt[:, 128:256]
    pl.semaphore_wait(barrier, len(peers))

    sent = []
    mid_copy = remote(mid_send.at[1], mid_recv, p_send.at[0], p_recv.at[0], pair, f)
    mid_copy.start()
    near = pl.ds(pl.multiple_of(512 * k, 512), 512)
    out_copy = remote(ox_ref.at[1], attn_ref.at[:, near], p_send.at[1], p_recv.at[1], pair, f)
    out_copy.start()
    attn_ref[:, near] = ox_ref[0]

    lowt = jnp.concatenate([lowx_ref[0], lowx_ref[1]], axis=1)
    upg = ADAPTER_SCALE * jnp.dot(lowt, glx, preferred_element_type=F32)
    buf[64:96] = jnp.zeros((32, 8, 128), F32)
    for s in range(2):
        for t in range(4):
            buf[64 + 16 * s + 8 * f + 4 * k + t] = upg[8 * s : 8 * s + 8, 128 * t : 128 * t + 128]
    mid_copy.wait()
    mid = (mid_send[0] + mid_recv[...]).astype(BF16)
    for t in range(4):
        part = jnp.dot(mid, normed_ref[:, 1024 * t : 1024 * t + 1024], preferred_element_type=F32)
        for s in range(2):
            for w in range(8):
                buf[32 * s + 8 * t + w] = part[8 * s : 8 * s + 8, 128 * w : 128 * w + 128]

    core_copy = remote(buf.at[pl.ds(48 * i, 48)], rcore, p_send.at[2], p_recv.at[2], sibling, f)
    core_copy.start()
    core_copy.wait()
    b1[...] = buf[pl.ds(48 * j, 48)] + rcore[...]
    copies = []
    for n, p in enumerate(xs):
        copy = remote(b1.at[pl.ds(12 * p, 12)], rx.at[n], x_send.at[n], x_recv.at[n], ctx_of(p, y, z, j), f)
        copy.start()
        copies.append(copy)
    for copy in copies:
        copy.wait()
    b2[...] = b1[pl.ds(12 * x, 12)] + rx[0] + rx[1] + rx[2]
    copies = []
    for n, p in enumerate(ys):
        copy = remote(b2.at[pl.ds(3 * p, 3)], ry.at[n], y_send.at[n], y_recv.at[n], ctx_of(x, p, z, j), f)
        copy.start()
        copies.append(copy)
    for copy in copies:
        copy.wait()
    b3[...] = b2[pl.ds(3 * y, 3)] + ry[0] + ry[1] + ry[2]
    copies = []
    for n, p in enumerate(zs):
        copy = remote(b3, rz.at[whole_z], z_send.at[n], z_recv.at[n], ctx_of(x, y, p % 4, j), p // 4)
        copy.start()
        copies.append(copy)
    rz[whole_z] = b3[...]
    for n, copy in enumerate(copies):
        source = (whole_z + 7 - n) % 8
        remote(rz.at[source], rz.at[source], z_send.at[n], z_recv.at[n], sibling, f).wait_recv()
    added = rz[0]
    for n in range(1, 8):
        added = added + rz[n]
    row = 48 * j + 12 * x + 3 * y
    final[pl.ds(row, 3)] = added
    sent += copies

    for n, p in enumerate(ys):
        part = final.at[pl.ds(row, 3)]
        copy = remote(part, part, gy_send.at[n], gy_recv.at[n], ctx_of(x, p, z, j), f)
        copy.start()
        sent.append(copy)
    for n in range(3):
        part = final.at[pl.ds(48 * j + 12 * x + 3 * ((y + 3 - n) % 4), 3)]
        remote(part, part, gy_send.at[n], gy_recv.at[n], sibling, f).wait_recv()
    for n, p in enumerate(xs):
        part = final.at[pl.ds(48 * j + 12 * x, 12)]
        copy = remote(part, part, gx_send.at[n], gx_recv.at[n], ctx_of(p, y, z, j), f)
        copy.start()
        sent.append(copy)
    for n in range(3):
        part = final.at[pl.ds(48 * j + 12 * ((x + 3 - n) % 4), 12)]
        remote(part, part, gx_send.at[n], gx_recv.at[n], sibling, f).wait_recv()
    part = final.at[pl.ds(48 * j, 48)]
    copy = remote(part, part, p_send.at[3], p_recv.at[3], sibling, f)
    copy.start()
    sent.append(copy)
    part = final.at[pl.ds(48 * i, 48)]
    remote(part, part, p_send.at[3], p_recv.at[3], sibling, f).wait_recv()

    for s in range(2):
        for t in range(32):
            grad_at_ref[8 * s : 8 * s + 8, 128 * t : 128 * t + 128] = final[32 * s + t]
        for t in range(8):
            up_out_ref[8 * s : 8 * s + 8, 128 * t : 128 * t + 128] = final[64 + 16 * s + 8 * f + t]

    other_half = attn_ref.at[:, pl.ds(pl.multiple_of(512 * (1 - k), 512), 512)]
    remote(ox_ref.at[1], other_half, p_send.at[1], p_recv.at[1], sibling, f).wait_recv()
    out_copy.wait_send()
    for copy in sent:
        copy.wait_send()


def reduce_all(ox, glx, lowx, normed, up):
    vmem = pl.BlockSpec(memory_space=pltpu.VMEM)
    hbm = pl.BlockSpec(memory_space=pl.ANY)
    dma = pltpu.SemaphoreType.DMA
    tiles = lambda *lead: pltpu.VMEM((*lead, 8, 128), F32)
    return pl.pallas_call(
        reduce_kernel,
        name="reduce_all",
        out_shape=(
            jax.ShapeDtypeStruct((128, 1024), BF16),
            jax.ShapeDtypeStruct((16, 4096), F32),
            jax.ShapeDtypeStruct((16, 1024), F32),
        ),
        in_specs=[vmem] * 5,
        out_specs=(vmem, vmem, vmem),
        scratch_shapes=[
            pltpu.VMEM((2, 16, 128), F32),
            pltpu.VMEM((16, 128), F32),
            tiles(96), tiles(48), tiles(48), tiles(3, 12), tiles(12), tiles(3, 3), tiles(3), tiles(8, 3),
            tiles(96),
        ]
        + [dma((n,)) for n in (4, 4, 3, 3, 3, 3, 7, 7, 3, 3, 3, 3)],
        compiler_params=pltpu.CompilerParams(
            collective_id=2, has_side_effects=True, vmem_limit_bytes=VMEM_LIMIT
        ),
    )(ox, glx, lowx, normed, up)


def on_device(
    layer_input,
    gain,
    codes,
    column_scale_quantized,
    block_second_scale,
    query_down_map,
    query_up_map,
    token_document,
    output_cotangent,
):
    x, y, z, j, _ = places()
    places_two = jnp.stack([ctx_of(x, y, z, j), pair_of(x, y, z, j)])
    freqs = jnp.exp(jnp.arange(HEAD // 2, dtype=F32) * (-2.0 * math.log(ROPE_BASE) / HEAD))
    positions = (places_two[:, None] * 128 + jnp.arange(128, dtype=I32)[None, :]).astype(F32)
    angle = positions[:, None, :] * freqs[None, :, None]
    cosine, sine = jnp.cos(angle), jnp.sin(angle)
    table = jnp.asarray(NF4_LEVELS * 8, F32)[None, :]

    q, kv, normed, lowt, ids, dox = project(
        layer_input,
        gain[None, :],
        codes,
        column_scale_quantized,
        block_second_scale[None, :],
        query_down_map.T,
        query_up_map,
        cosine,
        sine,
        table,
        token_document[None, :],
        output_cotangent,
    )
    qx, kvg, idg, lowx = gather(q, kv, lowt, ids)
    ox, glx = attend(qx, dox, kvg, idg, cosine, sine)
    attn, grad_at, up_map_gradient = reduce_all(ox, glx, lowx, normed, query_up_map)
    return (attn, grad_at.T, up_map_gradient)


def solution(mesh):
    return jax.shard_map(
        on_device,
        mesh=mesh,
        in_specs=(
            P("ctx", None),
            P(),
            P("fsdp", None),
            P("fsdp", None),
            P(),
            P(),
            P(None, "fsdp"),
            P("ctx"),
            P("ctx", "fsdp"),
        ),
        out_specs=(P("ctx", "fsdp"), P(), P(None, "fsdp")),
        check_vma=False,
    )
```

time: 222 us -> 165 us (0.74)
  Pallas kernels: 212 us -> 157 us
  local copies, waits for them, and re-layouts: 8.9 us -> 4.81 us
    pallas_call x1, Pallas kernels: 96.5 us -> 39.8 us  [reduce_all(): pl.pallas_call(reduce_kernel, name='reduce_all', out_shape=(jax.ShapeDtyp...]
    pallas_call x1, Pallas kernels: 67.3 us -> 46.2 us  [gather(): pl.pallas_call(gather_kernel, name='gather', out_shape=(jax.ShapeDtypeStr...]
    pallas_call x1, Pallas kernels: 6.84 us -> 25.3 us  [attend(): pl.pallas_call(attend_kernel, name='attend', out_shape=(jax.ShapeDtypeStr...]
    pallas_call x1, Pallas kernels: 41.3 us -> 45.6 us  [project(): pl.pallas_call(project_kernel, name='project', out_shape=(jax.ShapeDtypeS...]
    broadcast_in_dim x2 -> x0, local copies, waits for them, and re-layouts: 2.6 us -> none  [the longest x1 1.36 us: on_device(): block_second_scale[:, None]]
    unnamed x7 -> x3, local copies, waits for them, and re-layouts: 4.82 us -> 4.81 us
where the time goes in v2:
time: 165 us; the launch traced here: 164 us
  Pallas kernels  157 us (95%)
  local copies, waits for them, and re-layouts  4.81 us (3%)
    pallas_call x1, Pallas kernels, gather(): pl.pallas_call(gather_kernel, name='gather', out_shape=(jax.ShapeDtypeStr...  46.2 us
    pallas_call x1, Pallas kernels, project(): pl.pallas_call(project_kernel, name='project', out_shape=(jax.ShapeDtypeS...  45.6 us
    pallas_call x1, Pallas kernels, reduce_all(): pl.pallas_call(reduce_kernel, name='reduce_all', out_shape=(jax.ShapeDtyp...  39.8 us
    pallas_call x1, Pallas kernels, attend(): pl.pallas_call(attend_kernel, name='attend', out_shape=(jax.ShapeDtypeStr...  25.3 us
    unnamed x3, local copies, waits for them, and re-layouts  4.81 us

profile of v2, /device:TPU:1, one launch (start us, length us, event | category | flops | bytes accessed | tf_op | source)
XLA Modules:
  0.0 163.6 jit_solution(16105200010219507362)
XLA Ops:
  0.7 0.1 add_multiply_fusion
  0.8 0.1 add_convert_fusion
  0.9 1.0 multiply_sine_fusion
  1.8 45.6 %project.1 = (bf16[128,1024]{1,0:T(8,128)(2,1)}, bf16[2,128,256]{2,1,0:T(8,128)(2,1)}, bf16[128,4096]{1,0:T(8,128)(2,1)}, bf16[16,128]{1,0:T(8,128)(2,1)}, s32[8...) custom-call(bf16[128,4096]{1,0:T(8,128)(2,1)} %x_ref.1, f32[1,4096]{1,0:T(1,128)} %bitcast.9, s32[2048,384]{1,0:T(8,128)} %codes_ref.1, ...), custom_call_target="tpu_custom_call" | custom-call | tf_op jit(solution)/shard_map/project/pallas_call | solution.py:186
  47.4 46.2 %gather.1 = (bf16[2,128,512]{2,1,0:T(8,128)(2,1)}, bf16[2,64,128,256]{3,2,1,0:T(8,128)(2,1)}, s32[2,64,8,128]{3,2,1,0:T(8,128)}, bf16[2,16,128]{2,1,0:T(8,128)(2,1)}) custom-call(bf16[128,1024]{1,0:T(8,128)(2,1)} %get-tuple-element.18.q_ref, bf16[2,128,256]{2,1,0:T(8,128)(2,1)} %get-tuple-element.19.kv_ref, bf16[16,128]{1,0:T(8,128)(2,1)} %get-tuple-element.20.lowt_ref, ...), custom_call_target="tpu_custom_call" | custom-call | tf_op jit(solution)/shard_map/gather/pallas_call | solution.py:401
  93.7 25.3 %attend.1 = (bf16[2,128,512]{2,1,0:T(8,128)(2,1)}, bf16[2,128,512]{2,1,0:T(8,128)(2,1)}) custom-call(bf16[2,128,512]{2,1,0:T(8,128)(2,1)} %get-tuple-element.22.qx_ref, bf16[2,128,512]{2,1,0:T(8,128)(2,1)} %get-tuple-element.23.dox_ref, bf16[2,64,128,256]{3,2,1,0:T(8,128)(2,1)} %get-tuple-element.24.kvg_ref, s32[2,64,8,128]{3,2,1,0:T(8,128)} %get-tuple-element.25.idg_ref, ...), custom_call_target="tpu_custom_call" | custom-call | tf_op jit(solution)/shard_map/attend/pallas_call | solution.py:554
  119.0 39.8 %reduce_all.1 = (bf16[128,1024]{1,0:T(8,128)(2,1)}, f32[16,4096]{1,0:T(8,128)}, f32[16,1024]{1,0:T(8,128)}) custom-call(bf16[2,128,512]{2,1,0:T(8,128)(2,1)} %get-tuple-element.26.ox_ref, bf16[2,128,512]{2,1,0:T(8,128)(2,1)} %get-tuple-element.27.glx_ref, bf16[2,16,128]{2,1,0:T(8,128)(2,1)} %get-tuple-element.28.lowx_ref, ...), custom_call_target="tpu_custom_call" | custom-call | tf_op jit(solution)/shard_map/reduce_all/pallas_call | solution.py:710
  158.8 1.7 %copy.16 = bf16[128,1024]{1,0:T(8,128)(2,1)} copy(bf16[128,1024]{1,0:T(8,128)(2,1)} %get-tuple-element.38) | data formatting | bytes 524288
  160.5 1.7 %copy.17 = f32[4096,16]{0,1:T(8,128)} copy(f32[4096,16]{0,1:T(8,128)} %bitcast.7) | data formatting | bytes 524288
  162.2 1.5 copy.18
  (1 shorter events, 0.0 us)

commit v3 on v2

--- a/solution.py
+++ b/solution.py
@@ -74,33 +74,70 @@
 
 def project_kernel(
     x_ref, gain_ref, codes_ref, sq_ref, bs_ref, downt_ref, up_ref, cos_ref, sin_ref, table_ref, doc_ref, do_ref,
-    q_ref, kv_ref, normed_ref, lowt_ref, ids_ref, dox,
-    perm, scale, w_buf, acc, nat, send_main, send_half, recv_main, recv_half, total, send_sem, recv_sem,
+    normed_ref, dox, qx, kvg, idg, lowx,
+    perm, scale, w_buf, acc, parts, send_kv, recv_kv, send_q, recv_q, extra, kv_buf, q_buf, low_buf, ids_buf,
+    p_send, p_recv, e_send, e_recv, own_sem, z_send, z_recv, zi_send, zi_recv, a_send, a_recv, ai_send, ai_recv,
+    b_send, b_recv, bi_send, bi_recv, s_send, s_recv,
 ):
     x, y, z, j, f = places()
-    c = lax.axis_index("ctx")
+    here = lax.axis_index("ctx")
     other = 1 - f
+    i = 1 - j
+    k = z // 2
+    u = x * i + y * j
+    v = y * i + x * j
+
+    def at(uu, vv, zz):
+        return ctx_of(uu * i + vv * j, vv * i + uu * j, zz, j)
+
+    def slot(uu, vv, zz):
+        return (uu * 4 + vv) * 4 + zz
+
+    sibling = ctx_of(x, y, z, i)
     pair = pair_of(x, y, z, j)
-    k = z // 2
+    zo = (z + 2) % 4
+    zn = z + 1 - 2 * (z % 2)
+    zf = (zn + 2) % 4
+    across, next_z, far_z = at(u, v, zo), at(u, v, zn), at(u, v, zf)
+    vr, vl, vo = (v + 1) % 4, (v + 3) % 4, (v + 2) % 4
+    ur, ul, uo = (u + 1) % 4, (u + 3) % 4, (u + 2) % 4
+    right_v, left_v = at(u, vr, z), at(u, vl, z)
+    right_u, left_u = at(ur, v, z), at(ul, v, z)
+
     barrier = pltpu.get_barrier_semaphore()
-    pl.semaphore_signal(barrier, inc=1, device_id=(c, other), device_id_type=MESH)
-    pl.semaphore_signal(barrier, inc=1, device_id=(pair, f), device_id_type=MESH)
+    pl.semaphore_signal(barrier, inc=1, device_id=(here, other), device_id_type=MESH)
+    peers = [sibling, pair, across, next_z, far_z, right_v, left_v, right_u, left_u]
+    for peer in peers:
+        pl.semaphore_signal(barrier, inc=1, device_id=(peer, f), device_id_type=MESH)
 
     wide = x_ref[...].astype(F32)
     inverse = lax.rsqrt(jnp.mean(wide * wide, axis=-1, keepdims=True) + 1e-05)
     normed_ref[...] = (wide * inverse * gain_ref[...]).astype(BF16)
-    ids_ref[...] = jnp.broadcast_to(doc_ref[...], (8, 128))
-    dox[0] = do_ref[:, pl.ds(pl.multiple_of(512 * k, 512), 512)]
-
-    pl.semaphore_wait(barrier, 2)
+    ids_buf[...] = jnp.broadcast_to(doc_ref[...], (8, 128))
+    near = pl.ds(pl.multiple_of(512 * k, 512), 512)
     far = pl.ds(pl.multiple_of(512 * (1 - k), 512), 512)
-    copy_do = remote(do_ref.at[:, far], dox.at[1], send_sem.at[2], recv_sem.at[2], pair, f)
-    copy_do.start()
+    dox[0] = do_ref[:, near]
+
+    sent = []
+
+    def push(src, dst, n, send, recv, peer, group=f):
+        copy = remote(src, dst, send.at[n], recv.at[n], peer, group)
+        copy.start()
+        sent.append(copy)
+
+    def got(ref, n, send, recv):
+        remote(ref, ref, send.at[n], recv.at[n], sibling, f).wait_recv()
+
+    mine = slot(u, v, z)
+    pl.semaphore_wait(barrier, len(peers) + 1)
+    push(do_ref.at[:, far], dox.at[1], 3, e_send, e_recv, pair)
+    for n, peer in enumerate((next_z, across, far_z)):
+        push(ids_buf, idg.at[j, mine], n, zi_send, zi_recv, peer)
 
     for part in range(8):
         m = lax.broadcasted_iota(I32, (128, 1024), 0)
-        k = lax.broadcasted_iota(I32, (128, 1024), 1)
-        perm[128 * part : 128 * part + 128, :] = jnp.where(k == 8 * m + part, 1.0, 0.0).astype(BF16)
+        column = lax.broadcasted_iota(I32, (128, 1024), 1)
+        perm[128 * part : 128 * part + 128, :] = jnp.where(column == 8 * m + part, 1.0, 0.0).astype(BF16)
     pick = lax.broadcasted_iota(I32, (32, 64), 1) == lax.broadcasted_iota(I32, (32, 64), 0) + 32 * f
     second = jnp.sum(jnp.where(pick, bs_ref[...], 0.0), axis=1, keepdims=True) * (1.0 / 256.0)
     for t in range(3):
@@ -133,159 +170,60 @@
         full = acc[...]
         high = full.astype(BF16)
         low = (full - high.astype(F32)).astype(BF16)
-        nat[...] = jnp.dot(high, perm[...], preferred_element_type=F32) + jnp.dot(
+        parts[t] = jnp.dot(high, perm[...], preferred_element_type=F32) + jnp.dot(
             low, perm[...], preferred_element_type=F32
         )
 
-    own_main = pl.ds(pl.multiple_of(512 * f, 512), 1024)
-    own_half = pl.ds(pl.multiple_of(1024 * (1 - f), 512), 512)
-
-    tile(2 * (1 - f))
-    send_main[...] = nat[...].astype(BF16)
-    copy_main = remote(send_main, recv_main, send_sem.at[0], recv_sem.at[0], c, other)
-    copy_main.start()
-    tile(1)
-    send_half[...] = nat[:, pl.ds(pl.multiple_of(512 * (1 - f), 512), 512)].astype(BF16)
-    copy_half = remote(send_half, recv_half, send_sem.at[1], recv_sem.at[1], c, other)
-    copy_half.start()
-    total[:, own_half] = nat[:, pl.ds(pl.multiple_of(512 * f, 512), 512)]
-    tile(2 * f)
-    total[:, own_main] = nat[...]
+    def columns(t, offset):
+        return parts[t, :, pl.ds(pl.multiple_of(offset, 512), 512)]
+
+    tile(2 - f)
+    send_kv[...] = columns(2 - f, 512 * other).astype(BF16)
+    push(send_kv, recv_kv, 0, p_send, p_recv, here, other)
+    tile(1 + f)
+    tile(0)
+    send_q[:, 0:512] = columns(other, 512 * other).astype(BF16)
+    send_q[:, 512:1024] = columns(2 * other, 512 * f).astype(BF16)
+
+    cosine, sine = cos_ref[0].T, sin_ref[0].T
+    cosine = jnp.concatenate([cosine, cosine], axis=1)
+    sine = jnp.concatenate([-sine, sine], axis=1)
+
+    def rotate(vector):
+        return vector * cosine + pltpu.roll(vector, 64, 1) * sine
+
+    got(recv_kv, 0, p_send, p_recv)
+    both = columns(1 + f, 512 * f) + recv_kv[...].astype(F32)
+    for h in range(2):
+        kv_buf[h, :, 0:128] = rotate(both[:, 128 * h : 128 * h + 128]).astype(BF16)
+        kv_buf[h, :, 128:256] = both[:, 256 + 128 * h : 384 + 128 * h].astype(BF16)
+
+    push(kv_buf.at[1 - k], kvg.at[j, mine], 0, e_send, e_recv, across)
+    push(kv_buf.at[k], kvg.at[j, mine], 0, z_send, z_recv, next_z)
+    local = []
+
+    def keep(src, dst, n):
+        copy = pltpu.make_async_copy(src, dst, own_sem.at[n])
+        copy.start()
+        local.append(copy)
+
+    keep(kv_buf.at[k], kvg.at[j, mine], 0)
+    keep(ids_buf, idg.at[j, mine], 1)
 
     lowt = lax.dot_general(
         downt_ref[...], normed_ref[...], (((1,), (1,)), ((), ())), preferred_element_type=F32
     ).astype(BF16)
-    lowt_ref[...] = lowt
-    nat[...] = ADAPTER_SCALE * lax.dot_general(
+    low_buf[...] = lowt
+    extra[...] = ADAPTER_SCALE * lax.dot_general(
         lowt, up_ref[...], (((0,), (0,)), ((), ())), preferred_element_type=F32
     )
 
-    copy_main.wait()
-    total[:, own_main] += recv_main[...].astype(F32)
-    copy_half.wait()
-    total[:, own_half] += recv_half[...].astype(F32)
-
-    cosine, sine = cos_ref[0].T, sin_ref[0].T
-    cosine = jnp.concatenate([cosine, cosine], axis=1)
-    sine = jnp.concatenate([-sine, sine], axis=1)
-
-    def rotate(v):
-        return v * cosine + pltpu.roll(v, 64, 1) * sine
-
-    for h in range(8):
-        s = slice(128 * h, 128 * h + 128)
-        q_ref[:, s] = (rotate(total[:, s] + nat[:, s]) * QUERY_SCALE).astype(BF16)
-    for h in range(2):
-        kv_ref[h, :, 0:128] = rotate(total[:, 1024 + 128 * h : 1152 + 128 * h]).astype(BF16)
-        kv_ref[h, :, 128:256] = total[:, 1280 + 128 * h : 1408 + 128 * h].astype(BF16)
-    copy_do.wait()
-
-
-def project(x, gain, codes, sq, bs, downt, up, cosine, sine, table, doc, do):
-    vmem = pl.BlockSpec(memory_space=pltpu.VMEM)
-    return pl.pallas_call(
-        project_kernel,
-        name="project",
-        out_shape=(
-            jax.ShapeDtypeStruct((128, 1024), BF16),
-            jax.ShapeDtypeStruct((2, 128, 256), BF16),
-            jax.ShapeDtypeStruct((128, 4096), BF16),
-            jax.ShapeDtypeStruct((16, 128), BF16),
-            jax.ShapeDtypeStruct((8, 128), I32),
-            jax.ShapeDtypeStruct((2, 128, 512), BF16),
-        ),
-        in_specs=[vmem] * 12,
-        out_specs=(vmem,) * 6,
-        scratch_shapes=[
-            pltpu.VMEM((1024, 1024), BF16),
-            pltpu.VMEM((3, 32, 1024), F32),
-            pltpu.VMEM((256, 1024), BF16),
-            pltpu.VMEM((128, 1024), F32),
-            pltpu.VMEM((128, 1024), F32),
-            pltpu.VMEM((128, 1024), BF16),
-            pltpu.VMEM((128, 512), BF16),
-            pltpu.VMEM((128, 1024), BF16),
-            pltpu.VMEM((128, 512), BF16),
-            pltpu.VMEM((128, 1536), F32),
-            pltpu.SemaphoreType.DMA((3,)),
-            pltpu.SemaphoreType.DMA((3,)),
-        ],
-        compiler_params=pltpu.CompilerParams(
-            collective_id=0, has_side_effects=True, vmem_limit_bytes=VMEM_LIMIT
-        ),
-    )(x, gain, codes, sq, bs, downt, up, cosine, sine, table, doc, do)
-
-
-def gather_kernel(
-    q_ref, kv_ref, lowt_ref, ids_ref,
-    qx, kvg, idg, lowx,
-    e_send, e_recv, own_sem, z_send, z_recv, zi_send, zi_recv, a_send, a_recv, ai_send, ai_recv,
-    b_send, b_recv, bi_send, bi_recv, s_send, s_recv,
-):
-    x, y, z, j, f = places()
-    i = 1 - j
-    k = z // 2
-    u = x * i + y * j
-    v = y * i + x * j
-
-    def at(uu, vv, zz):
-        return ctx_of(uu * i + vv * j, vv * i + uu * j, zz, j)
-
-    def slot(uu, vv, zz):
-        return (uu * 4 + vv) * 4 + zz
-
-    sibling = ctx_of(x, y, z, i)
-    pair = pair_of(x, y, z, j)
-    zo = (z + 2) % 4
-    zn = z + 1 - 2 * (z % 2)
-    zf = (zn + 2) % 4
-    across, next_z, far_z = at(u, v, zo), at(u, v, zn), at(u, v, zf)
-    vr, vl, vo = (v + 1) % 4, (v + 3) % 4, (v + 2) % 4
-    ur, ul, uo = (u + 1) % 4, (u + 3) % 4, (u + 2) % 4
-    right_v, left_v = at(u, vr, z), at(u, vl, z)
-    right_u, left_u = at(ur, v, z), at(ul, v, z)
-
-    barrier = pltpu.get_barrier_semaphore()
-    peers = [sibling, pair, across, next_z, far_z, right_v, left_v, right_u, left_u]
-    for peer in peers:
-        pl.semaphore_signal(barrier, inc=1, device_id=(peer, f), device_id_type=MESH)
-    pl.semaphore_wait(barrier, len(peers))
-
-    sent = []
-
-    def push(src, dst, n, send, recv, peer):
-        copy = remote(src, dst, send.at[n], recv.at[n], peer, f)
-        copy.start()
-        sent.append(copy)
-
-    def got(ref, n, send, recv):
-        remote(ref, ref, send.at[n], recv.at[n], sibling, f).wait_recv()
-
-    mine = slot(u, v, z)
-    near = pl.ds(pl.multiple_of(512 * k, 512), 512)
-    far = pl.ds(pl.multiple_of(512 * (1 - k), 512), 512)
-    push(kv_ref.at[1 - k], kvg.at[j, mine], 0, e_send, e_recv, across)
-    push(kv_ref.at[k], kvg.at[j, mine], 0, z_send, z_recv, next_z)
-    for n, peer in enumerate((next_z, across, far_z)):
-        push(ids_ref, idg.at[j, mine], n, zi_send, zi_recv, peer)
-    push(q_ref.at[:, far], qx.at[1], 1, e_send, e_recv, pair)
-    push(lowt_ref, lowx.at[1], 2, e_send, e_recv, pair)
-    local = []
-    for n, (src, dst) in enumerate(
-        (
-            (kv_ref.at[k], kvg.at[j, mine]),
-            (ids_ref, idg.at[j, mine]),
-            (q_ref.at[:, near], qx.at[0]),
-            (lowt_ref, lowx.at[0]),
-        )
-    ):
-        copy = pltpu.make_async_copy(src, dst, own_sem.at[n])
-        copy.start()
-        local.append(copy)
-
-    second = kvg.at[j, slot(u, v, zo)]
-    got(second, 0, e_send, e_recv)
-    push(second, second, 1, z_send, z_recv, next_z)
+    block = kvg.at[j, slot(u, v, zo)]
+    got(block, 0, e_send, e_recv)
+    push(block, block, 1, z_send, z_recv, next_z)
+    push(send_q, recv_q, 1, p_send, p_recv, here, other)
+    push(low_buf, lowx.at[1], 2, e_send, e_recv, pair)
+    keep(low_buf, lowx.at[0], 2)
     got(kvg.at[j, slot(u, v, zn)], 0, z_send, z_recv)
     for n, zz in enumerate((zn, zo, zf)):
         got(idg.at[j, slot(u, v, zz)], n, zi_send, zi_recv)
@@ -354,6 +292,19 @@
     got(piece(ul, vl), 1, b_send, b_recv)
     same(piece(ul, vl), 9, b_send, b_recv, right_u)
     share(3, 3)
+
+    got(recv_q, 1, p_send, p_recv)
+    for h in range(8):
+        s = slice(128 * h, 128 * h + 128)
+        if h < 4:
+            own = parts[f, :, pl.ds(pl.multiple_of(512 * f + 128 * h, 128), 128)]
+        else:
+            own = parts[2 * f, :, pl.ds(pl.multiple_of(512 * other + 128 * (h - 4), 128), 128)]
+        whole = own + recv_q[:, s].astype(F32) + extra[:, s]
+        q_buf[:, s] = (rotate(whole) * QUERY_SCALE).astype(BF16)
+    push(q_buf.at[:, far], qx.at[1], 1, e_send, e_recv, pair)
+    keep(q_buf.at[:, near], qx.at[0], 3)
+
     got(piece(ur, vr), 6, b_send, b_recv)
     same(piece(ur, vr), 10, b_send, b_recv, left_u)
     share(1, 1)
@@ -382,8 +333,9 @@
     got(piece(uo, vo), 11, b_send, b_recv)
     share(2, 2)
 
+    got(dox.at[1], 3, e_send, e_recv)
+    got(lowx.at[1], 2, e_send, e_recv)
     got(qx.at[1], 1, e_send, e_recv)
-    got(lowx.at[1], 2, e_send, e_recv)
     for n, (du, dv) in enumerate(shared):
         got(kvg.at[i, pl.ds(slot((v + du) % 4, (u + dv) % 4, 0), 4)], n, s_send, s_recv)
     got(idg.at[i], 16, s_send, s_recv)
@@ -393,27 +345,45 @@
         copy.wait_send()
 
 
-def gather(q, kv, lowt, ids):
+def project(x, gain, codes, sq, bs, downt, up, cosine, sine, table, doc, do):
     vmem = pl.BlockSpec(memory_space=pltpu.VMEM)
     hbm = pl.BlockSpec(memory_space=pl.ANY)
     dma = pltpu.SemaphoreType.DMA
-    counts = (3, 3, 4, 2, 2, 3, 3, 6, 6, 3, 3, 12, 12, 3, 3, 17, 17)
+    counts = (2, 2, 4, 4, 4, 2, 2, 3, 3, 6, 6, 3, 3, 12, 12, 3, 3, 17, 17)
     return pl.pallas_call(
-        gather_kernel,
-        name="gather",
+        project_kernel,
+        name="project",
         out_shape=(
+            jax.ShapeDtypeStruct((128, 4096), BF16),
+            jax.ShapeDtypeStruct((2, 128, 512), BF16),
             jax.ShapeDtypeStruct((2, 128, 512), BF16),
             jax.ShapeDtypeStruct((2, 64, 128, 256), BF16),
             jax.ShapeDtypeStruct((2, 64, 8, 128), I32),
             jax.ShapeDtypeStruct((2, 16, 128), BF16),
         ),
-        in_specs=[vmem] * 4,
-        out_specs=(hbm,) * 4,
-        scratch_shapes=[dma((n,)) for n in counts],
+        in_specs=[vmem] * 12,
+        out_specs=(vmem, vmem, hbm, hbm, hbm, hbm),
+        scratch_shapes=[
+            pltpu.VMEM((1024, 1024), BF16),
+            pltpu.VMEM((3, 32, 1024), F32),
+            pltpu.VMEM((256, 1024), BF16),
+            pltpu.VMEM((128, 1024), F32),
+            pltpu.VMEM((3, 128, 1024), F32),
+            pltpu.VMEM((128, 512), BF16),
+            pltpu.VMEM((128, 512), BF16),
+            pltpu.VMEM((128, 1024), BF16),
+            pltpu.VMEM((128, 1024), BF16),
+            pltpu.VMEM((128, 1024), F32),
+            pltpu.VMEM((2, 128, 256), BF16),
+            pltpu.VMEM((128, 1024), BF16),
+            pltpu.VMEM((16, 128), BF16),
+            pltpu.VMEM((8, 128), I32),
+        ]
+        + [dma((n,)) for n in counts],
         compiler_params=pltpu.CompilerParams(
-            collective_id=1, has_side_effects=True, vmem_limit_bytes=VMEM_LIMIT
+            collective_id=0, has_side_effects=True, vmem_limit_bytes=VMEM_LIMIT
         ),
-    )(q, kv, lowt, ids)
+    )(x, gain, codes, sq, bs, downt, up, cosine, sine, table, doc, do)
 
 
 STEP = 512
@@ -577,15 +547,14 @@
 def reduce_kernel(
     ox_ref, glx_ref, lowx_ref, normed_ref, up_ref,
     attn_ref, grad_at_ref, up_out_ref,
-    mid_send, mid_recv, buf, rcore, b1, rx, b2, ry, b3, rz, final,
-    p_send, p_recv, x_send, x_recv, y_send, y_recv, z_send, z_recv,
-    gy_send, gy_recv, gx_send, gx_recv,
+    mid_send, mid_recv, buf, rcore, b1, rp, b3, rz, final,
+    p_send, p_recv, x_send, x_recv, z_send, z_recv, g_send, g_recv,
 ):
     x, y, z, j, f = places()
     i = 1 - j
     sibling = ctx_of(x, y, z, i)
-    xs = [(x + d) % 4 for d in (1, 2, 3)]
-    ys = [(y + d) % 4 for d in (1, 2, 3)]
+    flat = x * 4 + y
+    plane = [(flat + d) % 16 for d in range(1, 16)]
     whole_z = f * 4 + z
     zs = [(whole_z + d) % 8 for d in range(1, 8)]
 
@@ -593,8 +562,7 @@
     k = z // 2
     barrier = pltpu.get_barrier_semaphore()
     peers = [(sibling, f), (pair, f)]
-    peers += [(ctx_of(p, y, z, j), f) for p in xs]
-    peers += [(ctx_of(x, p, z, j), f) for p in ys]
+    peers += [(ctx_of(p // 4, p % 4, z, j), f) for p in plane]
     peers += [(ctx_of(x, y, p % 4, j), p // 4) for p in zs]
     for peer in peers:
         pl.semaphore_signal(barrier, inc=1, device_id=peer, device_id_type=MESH)
@@ -613,7 +581,6 @@
     mid_copy.start()
     near = pl.ds(pl.multiple_of(512 * k, 512), 512)
     out_copy = remote(ox_ref.at[1], attn_ref.at[:, near], p_send.at[1], p_recv.at[1], pair, f)
-    out_copy.start()
     attn_ref[:, near] = ox_ref[0]
 
     lowt = jnp.concatenate([lowx_ref[0], lowx_ref[1]], axis=1)
@@ -635,21 +602,17 @@
     core_copy.wait()
     b1[...] = buf[pl.ds(48 * j, 48)] + rcore[...]
     copies = []
-    for n, p in enumerate(xs):
-        copy = remote(b1.at[pl.ds(12 * p, 12)], rx.at[n], x_send.at[n], x_recv.at[n], ctx_of(p, y, z, j), f)
+    for n, p in enumerate(plane):
+        peer = ctx_of(p // 4, p % 4, z, j)
+        copy = remote(b1.at[pl.ds(3 * p, 3)], rp.at[n], x_send.at[n], x_recv.at[n], peer, f)
         copy.start()
         copies.append(copy)
-    for copy in copies:
+    out_copy.start()
+    added = b1[pl.ds(3 * flat, 3)]
+    for n, copy in enumerate(copies):
         copy.wait()
-    b2[...] = b1[pl.ds(12 * x, 12)] + rx[0] + rx[1] + rx[2]
-    copies = []
-    for n, p in enumerate(ys):
-        copy = remote(b2.at[pl.ds(3 * p, 3)], ry.at[n], y_send.at[n], y_recv.at[n], ctx_of(x, p, z, j), f)
-        copy.start()
-        copies.append(copy)
-    for copy in copies:
-        copy.wait()
-    b3[...] = b2[pl.ds(3 * y, 3)] + ry[0] + ry[1] + ry[2]
+        added = added + rp[n]
+    b3[...] = added
     copies = []
     for n, p in enumerate(zs):
         copy = remote(b3, rz.at[whole_z], z_send.at[n], z_recv.at[n], ctx_of(x, y, p % 4, j), p // 4)
@@ -662,26 +625,18 @@
     added = rz[0]
     for n in range(1, 8):
         added = added + rz[n]
-    row = 48 * j + 12 * x + 3 * y
+    row = 48 * j + 3 * flat
     final[pl.ds(row, 3)] = added
     sent += copies
 
-    for n, p in enumerate(ys):
+    for n, p in enumerate(plane):
         part = final.at[pl.ds(row, 3)]
-        copy = remote(part, part, gy_send.at[n], gy_recv.at[n], ctx_of(x, p, z, j), f)
+        copy = remote(part, part, g_send.at[n], g_recv.at[n], ctx_of(p // 4, p % 4, z, j), f)
         copy.start()
         sent.append(copy)
-    for n in range(3):
-        part = final.at[pl.ds(48 * j + 12 * x + 3 * ((y + 3 - n) % 4), 3)]
-        remote(part, part, gy_send.at[n], gy_recv.at[n], sibling, f).wait_recv()
-    for n, p in enumerate(xs):
-        part = final.at[pl.ds(48 * j + 12 * x, 12)]
-        copy = remote(part, part, gx_send.at[n], gx_recv.at[n], ctx_of(p, y, z, j), f)
-        copy.start()
-        sent.append(copy)
-    for n in range(3):
-        part = final.at[pl.ds(48 * j + 12 * ((x + 3 - n) % 4), 12)]
-        remote(part, part, gx_send.at[n], gx_recv.at[n], sibling, f).wait_recv()
+    for n in range(15):
+        part = final.at[pl.ds(48 * j + 3 * ((flat + 15 - n) % 16), 3)]
+        remote(part, part, g_send.at[n], g_recv.at[n], sibling, f).wait_recv()
     part = final.at[pl.ds(48 * j, 48)]
     copy = remote(part, part, p_send.at[3], p_recv.at[3], sibling, f)
     copy.start()
@@ -720,14 +675,32 @@
         scratch_shapes=[
             pltpu.VMEM((2, 16, 128), F32),
             pltpu.VMEM((16, 128), F32),
-            tiles(96), tiles(48), tiles(48), tiles(3, 12), tiles(12), tiles(3, 3), tiles(3), tiles(8, 3),
+            tiles(96), tiles(48), tiles(48), tiles(15, 3), tiles(3), tiles(8, 3),
             tiles(96),
         ]
-        + [dma((n,)) for n in (4, 4, 3, 3, 3, 3, 7, 7, 3, 3, 3, 3)],
+        + [dma((n,)) for n in (4, 4, 15, 15, 7, 7, 15, 15)],
         compiler_params=pltpu.CompilerParams(
-            collective_id=2, has_side_effects=True, vmem_limit_bytes=VMEM_LIMIT
+            collective_id=1, has_side_effects=True, vmem_limit_bytes=VMEM_LIMIT
         ),
     )(ox, glx, lowx, normed, up)
+
+
+def hand_over_kernel(a_ref, b_ref, c_ref, a_out, b_out, c_out):
+    a_out[...] = a_ref[...]
+    b_out[...] = b_ref[...]
+    c_out[...] = c_ref[...]
+
+
+def hand_over(*arrays):
+    vmem = pl.BlockSpec(memory_space=pltpu.VMEM)
+    return pl.pallas_call(
+        hand_over_kernel,
+        name="hand_over",
+        out_shape=tuple(jax.ShapeDtypeStruct(a.shape, a.dtype) for a in arrays),
+        in_specs=[vmem] * 3,
+        out_specs=(vmem,) * 3,
+        compiler_params=pltpu.CompilerParams(vmem_limit_bytes=VMEM_LIMIT),
+    )(*arrays)
 
 
 def on_device(
@@ -749,7 +722,7 @@
     cosine, sine = jnp.cos(angle), jnp.sin(angle)
     table = jnp.asarray(NF4_LEVELS * 8, F32)[None, :]
 
-    q, kv, normed, lowt, ids, dox = project(
+    normed, dox, qx, kvg, idg, lowx = project(
         layer_input,
         gain[None, :],
         codes,
@@ -763,9 +736,9 @@
         token_document[None, :],
         output_cotangent,
     )
-    qx, kvg, idg, lowx = gather(q, kv, lowt, ids)
     ox, glx = attend(qx, dox, kvg, idg, cosine, sine)
     attn, grad_at, up_map_gradient = reduce_all(ox, glx, lowx, normed, query_up_map)
+    attn, grad_at, up_map_gradient = hand_over(attn, grad_at, up_map_gradient)
     return (attn, grad_at.T, up_map_gradient)
 
 

time: 165 us -> 151 us (0.915); the launches traced: 164 us -> 152 us
  Pallas kernels: 157 us -> 150 us
  local copies, waits for them, and re-layouts: 4.81 us -> 0 us
    pallas_call x1, Pallas kernels: 46.2 us -> 1.85 us  [hand_over(): pl.pallas_call(hand_over_kernel, name='hand_over', out_shape=tuple((jax.S...]
    pallas_call x1, Pallas kernels: 45.6 us -> 89.9 us  [project(): pl.pallas_call(project_kernel, name='project', out_shape=(jax.ShapeDtypeS...]
    pallas_call x1, Pallas kernels: 25.3 us -> 8.84 us  [attend(): pl.pallas_call(attend_kernel, name='attend', out_shape=(jax.ShapeDtypeStr...]
    pallas_call x1, Pallas kernels: 39.8 us -> 49.4 us  [reduce_all(): pl.pallas_call(reduce_kernel, name='reduce_all', out_shape=(jax.ShapeDtyp...]
    unnamed x3 -> x0, local copies, waits for them, and re-layouts: 4.81 us -> none
where the time goes in v3:
time: 151 us; the launch traced here: 152 us
  Pallas kernels  150 us (99%)
    pallas_call x1, Pallas kernels, project(): pl.pallas_call(project_kernel, name='project', out_shape=(jax.ShapeDtypeS...  89.9 us
    pallas_call x1, Pallas kernels, reduce_all(): pl.pallas_call(reduce_kernel, name='reduce_all', out_shape=(jax.ShapeDtyp...  49.4 us
    pallas_call x1, Pallas kernels, attend(): pl.pallas_call(attend_kernel, name='attend', out_shape=(jax.ShapeDtypeStr...  8.84 us

profile of v3, /device:TPU:1, one launch (start us, length us, event | category | flops | bytes accessed | tf_op | source)
XLA Modules:
  0.0 151.8 jit_solution(4566792286768124751)
XLA Ops:
  0.7 0.1 add_multiply_fusion
  0.8 0.1 add_convert_fusion
  0.9 1.0 multiply_sine_fusion
  1.8 89.9 %project.1 = (bf16[128,4096]{1,0:T(8,128)(2,1)}, bf16[2,128,512]{2,1,0:T(8,128)(2,1)}, bf16[2,128,512]{2,1,0:T(8,128)(2,1)}, bf16[2,64,128,256]{3,2,1,0:T(8,128)...) custom-call(bf16[128,4096]{1,0:T(8,128)(2,1)} %x_ref.1, f32[1,4096]{1,0:T(1,128)} %bitcast.8, ...), custom_call_target="tpu_custom_call" | custom-call | tf_op jit(solution)/shard_map/project/pallas_call | solution.py:353
  91.7 8.8 %attend.1 = (bf16[2,128,512]{2,1,0:T(8,128)(2,1)}, bf16[2,128,512]{2,1,0:T(8,128)(2,1)}) custom-call(bf16[2,128,512]{2,1,0:T(8,128)(2,1)} %get-tuple-element.17.qx_ref, bf16[2,128,512]{2,1,0:T(8,128)(2,1)} %get-tuple-element.18.dox_ref, bf16[2,64,128,256]{3,2,1,0:T(8,128)(2,1)} %get-tuple-element.19.kvg_ref, s32[2,64,8,128]{3,2,1,0:T(8,128)} %get-tuple-element.20.idg_ref, ...), custom_call_target="tpu_custom_call" | custom-call | tf_op jit(solution)/shard_map/attend/pallas_call | solution.py:524
  100.6 49.4 %reduce_all.1 = (bf16[128,1024]{1,0:T(8,128)(2,1)}, f32[16,4096]{1,0:T(8,128)}, f32[16,1024]{1,0:T(8,128)}) custom-call(bf16[2,128,512]{2,1,0:T(8,128)(2,1)} %get-tuple-element.21.ox_ref, bf16[2,128,512]{2,1,0:T(8,128)(2,1)} %get-tuple-element.22.glx_ref, bf16[2,16,128]{2,1,0:T(8,128)(2,1)} %get-tuple-element.23.lowx_ref, ...), custom_call_target="tpu_custom_call" | custom-call | tf_op jit(solution)/shard_map/reduce_all/pallas_call | solution.py:665
  150.0 1.9 %hand_over.1 = (bf16[128,1024]{1,0:T(8,128)(2,1)}, f32[16,4096]{1,0:T(8,128)}, f32[16,1024]{1,0:T(8,128)}) custom-call(bf16[128,1024]{1,0:T(8,128)(2,1)} %get-tuple-element.25.a_ref, f32[16,4096]{1,0:T(8,128)} %get-tuple-element.26.b_ref, f32[16,1024]{1,0:T(8,128)} %get-tuple-element.27.c_ref), custom_call_target="tpu_custom_call" | custom-call | tf_op jit(solution)/shard_map/hand_over/pallas_call | solution.py:696
  (1 shorter events, 0.0 us)

commit v4 on v3

--- a/solution.py
+++ b/solution.py
@@ -56,10 +56,10 @@
         index[..., None],
         lax.GatherDimensionNumbers(
             offset_dims=(),
-            collapsed_slice_dims=(1,),
-            start_index_map=(1,),
-            operand_batching_dims=(0,),
-            start_indices_batching_dims=(0,),
+            collapsed_slice_dims=(0,),
+            start_index_map=(0,),
+            operand_batching_dims=(1,),
+            start_indices_batching_dims=(1,),
         ),
         slice_sizes=(1, 1),
         mode=lax.GatherScatterMode.PROMISE_IN_BOUNDS,
@@ -145,7 +145,7 @@
         packed = lax.dot_general(quantized, perm[...], (((1,), (1,)), ((), ())), preferred_element_type=F32)
         scale[t] = packed * second
 
-    table = jnp.broadcast_to(table_ref[...], (64, 128))
+    lower, upper = table_ref[0:8, :], table_ref[8:16, :]
 
     def tile(t):
         lane = pl.multiple_of(t * 128, 128)
@@ -157,10 +157,14 @@
                 words = codes_ref[pl.ds(row, 64), pl.ds(lane, 128)]
                 scale_row = scale[t, pl.ds(kc * 4 + b, 1), :]
                 for n in range(8):
-                    index = jnp.bitwise_and(jnp.right_shift(words, 4 * n), 15)
-                    levels = lookup(table, index)
+                    rows = []
+                    for r in range(8):
+                        word = words[8 * r : 8 * r + 8]
+                        index = jnp.bitwise_and(jnp.right_shift(word, 4 * n), 7)
+                        high = jnp.left_shift(word, 28 - 4 * n) < 0
+                        rows.append(jnp.where(high, lookup(upper, index), lookup(lower, index)))
                     w_buf[64 * b : 64 * b + 64, 128 * n : 128 * n + 128] = (
-                        levels * scale_row[:, 128 * n : 128 * n + 128]
+                        jnp.concatenate(rows, axis=0) * scale_row[:, 128 * n : 128 * n + 128]
                     ).astype(BF16)
             col = pl.multiple_of(f * 2048 + kc * 256, 256)
             acc[...] += jnp.dot(normed_ref[:, pl.ds(col, 256)], w_buf[...], preferred_element_type=F32)
@@ -720,7 +724,7 @@
     positions = (places_two[:, None] * 128 + jnp.arange(128, dtype=I32)[None, :]).astype(F32)
     angle = positions[:, None, :] * freqs[None, :, None]
     cosine, sine = jnp.cos(angle), jnp.sin(angle)
-    table = jnp.asarray(NF4_LEVELS * 8, F32)[None, :]
+    table = jnp.broadcast_to(jnp.asarray(NF4_LEVELS, F32)[:, None], (16, 128))
 
     normed, dox, qx, kvg, idg, lowx = project(
         layer_input,

time: 151 us -> 143 us (0.947)
  Pallas kernels: 150 us -> 140 us
    pallas_call x1, Pallas kernels: 89.9 us -> 78.6 us  [project(): pl.pallas_call(project_kernel, name='project', out_shape=(jax.ShapeDtypeS...]
where the time goes in v4:
time: 143 us
  Pallas kernels  140 us (98%)
    pallas_call x1, Pallas kernels, project(): pl.pallas_call(project_kernel, name='project', out_shape=(jax.ShapeDtypeS...  78.6 us
    pallas_call x1, Pallas kernels, reduce_all(): pl.pallas_call(reduce_kernel, name='reduce_all', out_shape=(jax.ShapeDtyp...  48.9 us
    pallas_call x1, Pallas kernels, attend(): pl.pallas_call(attend_kernel, name='attend', out_shape=(jax.ShapeDtypeStr...  10.3 us

profile of v4, /device:TPU:1, one launch (start us, length us, event | category | flops | bytes accessed | tf_op | source)
XLA Modules:
  0.0 142.9 jit_solution(15503897089344690924)
XLA Ops:
  0.7 0.1 add_multiply_fusion
  0.8 0.1 add_convert_fusion
  0.9 1.0 multiply_sine_fusion
  1.8 1.3 broadcast_in_dim.10.table_ref
  3.2 78.6 %project.1 = (bf16[128,4096]{1,0:T(8,128)(2,1)}, bf16[2,128,512]{2,1,0:T(8,128)(2,1)}, bf16[2,128,512]{2,1,0:T(8,128)(2,1)}, bf16[2,64,128,256]{3,2,1,0:T(8,128)...) custom-call(bf16[128,4096]{1,0:T(8,128)(2,1)} %x_ref.1, f32[1,4096]{1,0:T(1,128)} %bitcast.8, ...), custom_call_target="tpu_custom_call" | custom-call | tf_op jit(solution)/shard_map/project/pallas_call | solution.py:357
  81.8 10.3 %attend.1 = (bf16[2,128,512]{2,1,0:T(8,128)(2,1)}, bf16[2,128,512]{2,1,0:T(8,128)(2,1)}) custom-call(bf16[2,128,512]{2,1,0:T(8,128)(2,1)} %get-tuple-element.17.qx_ref, bf16[2,128,512]{2,1,0:T(8,128)(2,1)} %get-tuple-element.18.dox_ref, bf16[2,64,128,256]{3,2,1,0:T(8,128)(2,1)} %get-tuple-element.19.kvg_ref, s32[2,64,8,128]{3,2,1,0:T(8,128)} %get-tuple-element.20.idg_ref, ...), custom_call_target="tpu_custom_call" | custom-call | tf_op jit(solution)/shard_map/attend/pallas_call | solution.py:528
  92.1 48.9 %reduce_all.1 = (bf16[128,1024]{1,0:T(8,128)(2,1)}, f32[16,4096]{1,0:T(8,128)}, f32[16,1024]{1,0:T(8,128)}) custom-call(bf16[2,128,512]{2,1,0:T(8,128)(2,1)} %get-tuple-element.21.ox_ref, bf16[2,128,512]{2,1,0:T(8,128)(2,1)} %get-tuple-element.22.glx_ref, bf16[2,16,128]{2,1,0:T(8,128)(2,1)} %get-tuple-element.23.lowx_ref, ...), custom_call_target="tpu_custom_call" | custom-call | tf_op jit(solution)/shard_map/reduce_all/pallas_call | solution.py:669
  141.0 1.9 %hand_over.1 = (bf16[128,1024]{1,0:T(8,128)(2,1)}, f32[16,4096]{1,0:T(8,128)}, f32[16,1024]{1,0:T(8,128)}) custom-call(bf16[128,1024]{1,0:T(8,128)(2,1)} %get-tuple-element.25.a_ref, f32[16,4096]{1,0:T(8,128)} %get-tuple-element.26.b_ref, f32[16,1024]{1,0:T(8,128)} %get-tuple-element.27.c_ref), custom_call_target="tpu_custom_call" | custom-call | tf_op jit(solution)/shard_map/hand_over/pallas_call | solution.py:700
  (1 shorter events, 0.0 us)

commit v5 on v4

--- a/solution.py
+++ b/solution.py
@@ -3,6 +3,7 @@
 
 import jax
 import jax.numpy as jnp
+import numpy as np
 from jax import lax
 from jax.experimental import pallas as pl
 from jax.experimental.pallas import tpu as pltpu
@@ -110,9 +111,10 @@
     for peer in peers:
         pl.semaphore_signal(barrier, inc=1, device_id=(peer, f), device_id_type=MESH)
 
-    wide = x_ref[...].astype(F32)
-    inverse = lax.rsqrt(jnp.mean(wide * wide, axis=-1, keepdims=True) + 1e-05)
-    normed_ref[...] = (wide * inverse * gain_ref[...]).astype(BF16)
+    for r in range(8):
+        wide = x_ref[16 * r : 16 * r + 16, :].astype(F32)
+        inverse = lax.rsqrt(jnp.mean(wide * wide, axis=-1, keepdims=True) + 1e-05)
+        normed_ref[16 * r : 16 * r + 16, :] = (wide * inverse * gain_ref[...]).astype(BF16)
     ids_buf[...] = jnp.broadcast_to(doc_ref[...], (8, 128))
     near = pl.ds(pl.multiple_of(512 * k, 512), 512)
     far = pl.ds(pl.multiple_of(512 * (1 - k), 512), 512)
@@ -140,10 +142,15 @@
         perm[128 * part : 128 * part + 128, :] = jnp.where(column == 8 * m + part, 1.0, 0.0).astype(BF16)
     pick = lax.broadcasted_iota(I32, (32, 64), 1) == lax.broadcasted_iota(I32, (32, 64), 0) + 32 * f
     second = jnp.sum(jnp.where(pick, bs_ref[...], 0.0), axis=1, keepdims=True) * (1.0 / 256.0)
+    quantized = jnp.concatenate([sq_ref[:, 1024 * t : 1024 * t + 1024] for t in range(3)], axis=0)
+    packed = lax.dot_general(
+        (quantized.astype(F32) + 1.0).astype(BF16),
+        perm[...],
+        (((1,), (1,)), ((), ())),
+        preferred_element_type=F32,
+    )
     for t in range(3):
-        quantized = (sq_ref[:, 1024 * t : 1024 * t + 1024].astype(F32) + 1.0).astype(BF16)
-        packed = lax.dot_general(quantized, perm[...], (((1,), (1,)), ((), ())), preferred_element_type=F32)
-        scale[t] = packed * second
+        scale[t] = packed[32 * t : 32 * t + 32] * second
 
     lower, upper = table_ref[0:8, :], table_ref[8:16, :]
 
@@ -174,9 +181,8 @@
         full = acc[...]
         high = full.astype(BF16)
         low = (full - high.astype(F32)).astype(BF16)
-        parts[t] = jnp.dot(high, perm[...], preferred_element_type=F32) + jnp.dot(
-            low, perm[...], preferred_element_type=F32
-        )
+        natural = jnp.dot(jnp.concatenate([high, low], axis=0), perm[...], preferred_element_type=F32)
+        parts[t] = natural[0:128] + natural[128:256]
 
     def columns(t, offset):
         return parts[t, :, pl.ds(pl.multiple_of(offset, 512), 512)]
@@ -184,10 +190,10 @@
     tile(2 - f)
     send_kv[...] = columns(2 - f, 512 * other).astype(BF16)
     push(send_kv, recv_kv, 0, p_send, p_recv, here, other)
-    tile(1 + f)
-    tile(0)
+    tile(other)
     send_q[:, 0:512] = columns(other, 512 * other).astype(BF16)
     send_q[:, 512:1024] = columns(2 * other, 512 * f).astype(BF16)
+    tile(2 * f)
 
     cosine, sine = cos_ref[0].T, sin_ref[0].T
     cosine = jnp.concatenate([cosine, cosine], axis=1)
@@ -228,6 +234,7 @@
     push(send_q, recv_q, 1, p_send, p_recv, here, other)
     push(low_buf, lowx.at[1], 2, e_send, e_recv, pair)
     keep(low_buf, lowx.at[0], 2)
+
     got(kvg.at[j, slot(u, v, zn)], 0, z_send, z_recv)
     for n, zz in enumerate((zn, zo, zf)):
         got(idg.at[j, slot(u, v, zz)], n, zi_send, zi_recv)
@@ -724,7 +731,7 @@
     positions = (places_two[:, None] * 128 + jnp.arange(128, dtype=I32)[None, :]).astype(F32)
     angle = positions[:, None, :] * freqs[None, :, None]
     cosine, sine = jnp.cos(angle), jnp.sin(angle)
-    table = jnp.broadcast_to(jnp.asarray(NF4_LEVELS, F32)[:, None], (16, 128))
+    table = jnp.asarray(np.tile(np.asarray(NF4_LEVELS, np.float32)[:, None], (1, 128)))
 
     normed, dox, qx, kvg, idg, lowx = project(
         layer_input,

time: 143 us -> 140 us (0.979)
  no operation moved by 1% of the time
where the time goes in v5:
time: 140 us; the launch traced here: 141 us
  Pallas kernels  139 us (99%)
    pallas_call x1, Pallas kernels, project(): pl.pallas_call(project_kernel, name='project', out_shape=(jax.ShapeDtypeS...  77.5 us
    pallas_call x1, Pallas kernels, reduce_all(): pl.pallas_call(reduce_kernel, name='reduce_all', out_shape=(jax.ShapeDtyp...  49.1 us
    pallas_call x1, Pallas kernels, attend(): pl.pallas_call(attend_kernel, name='attend', out_shape=(jax.ShapeDtypeStr...  10.3 us

profile of v5, /device:TPU:1, one launch (start us, length us, event | category | flops | bytes accessed | tf_op | source)
XLA Modules:
  0.0 140.6 jit_solution(6617258072475235168)
XLA Ops:
  0.7 0.1 add_multiply_fusion
  0.8 0.1 add_convert_fusion
  0.9 1.0 multiply_sine_fusion
  1.8 77.5 %project.1 = (bf16[128,4096]{1,0:T(8,128)(2,1)}, bf16[2,128,512]{2,1,0:T(8,128)(2,1)}, bf16[2,128,512]{2,1,0:T(8,128)(2,1)}, bf16[2,64,128,256]{3,2,1,0:T(8,128)...) custom-call(bf16[128,4096]{1,0:T(8,128)(2,1)} %x_ref.1, f32[1,4096]{1,0:T(1,128)} %bitcast.8, ...), custom_call_target="tpu_custom_call" | custom-call | tf_op jit(solution)/shard_map/project/pallas_call | solution.py:364
  79.3 10.3 %attend.1 = (bf16[2,128,512]{2,1,0:T(8,128)(2,1)}, bf16[2,128,512]{2,1,0:T(8,128)(2,1)}) custom-call(bf16[2,128,512]{2,1,0:T(8,128)(2,1)} %get-tuple-element.17.qx_ref, bf16[2,128,512]{2,1,0:T(8,128)(2,1)} %get-tuple-element.18.dox_ref, bf16[2,64,128,256]{3,2,1,0:T(8,128)(2,1)} %get-tuple-element.19.kvg_ref, s32[2,64,8,128]{3,2,1,0:T(8,128)} %get-tuple-element.20.idg_ref, ...), custom_call_target="tpu_custom_call" | custom-call | tf_op jit(solution)/shard_map/attend/pallas_call | solution.py:535
  89.6 49.1 %reduce_all.1 = (bf16[128,1024]{1,0:T(8,128)(2,1)}, f32[16,4096]{1,0:T(8,128)}, f32[16,1024]{1,0:T(8,128)}) custom-call(bf16[2,128,512]{2,1,0:T(8,128)(2,1)} %get-tuple-element.21.ox_ref, bf16[2,128,512]{2,1,0:T(8,128)(2,1)} %get-tuple-element.22.glx_ref, bf16[2,16,128]{2,1,0:T(8,128)(2,1)} %get-tuple-element.23.lowx_ref, ...), custom_call_target="tpu_custom_call" | custom-call | tf_op jit(solution)/shard_map/reduce_all/pallas_call | solution.py:676
  138.8 1.9 %hand_over.1 = (bf16[128,1024]{1,0:T(8,128)(2,1)}, f32[16,4096]{1,0:T(8,128)}, f32[16,1024]{1,0:T(8,128)}) custom-call(bf16[128,1024]{1,0:T(8,128)(2,1)} %get-tuple-element.25.a_ref, f32[16,4096]{1,0:T(8,128)} %get-tuple-element.26.b_ref, f32[16,1024]{1,0:T(8,128)} %get-tuple-element.27.c_ref), custom_call_target="tpu_custom_call" | custom-call | tf_op jit(solution)/shard_map/hand_over/pallas_call | solution.py:707
  (1 shorter events, 0.0 us)

commit v6 on v5

--- a/solution.py
+++ b/solution.py
@@ -164,15 +164,15 @@
                 words = codes_ref[pl.ds(row, 64), pl.ds(lane, 128)]
                 scale_row = scale[t, pl.ds(kc * 4 + b, 1), :]
                 for n in range(8):
+                    scales = scale_row[:, 128 * n : 128 * n + 128]
+                    scaled_lower, scaled_upper = lower * scales, upper * scales
                     rows = []
                     for r in range(8):
                         word = words[8 * r : 8 * r + 8]
                         index = jnp.bitwise_and(jnp.right_shift(word, 4 * n), 7)
                         high = jnp.left_shift(word, 28 - 4 * n) < 0
-                        rows.append(jnp.where(high, lookup(upper, index), lookup(lower, index)))
-                    w_buf[64 * b : 64 * b + 64, 128 * n : 128 * n + 128] = (
-                        jnp.concatenate(rows, axis=0) * scale_row[:, 128 * n : 128 * n + 128]
-                    ).astype(BF16)
+                        rows.append(jnp.where(high, lookup(scaled_upper, index), lookup(scaled_lower, index)))
+                    w_buf[64 * b : 64 * b + 64, 128 * n : 128 * n + 128] = jnp.concatenate(rows, axis=0).astype(BF16)
             col = pl.multiple_of(f * 2048 + kc * 256, 256)
             acc[...] += jnp.dot(normed_ref[:, pl.ds(col, 256)], w_buf[...], preferred_element_type=F32)
             return carry

time: 140 us -> 138 us (0.986)
  Pallas kernels: 139 us -> 136 us
    pallas_call x1, Pallas kernels: 49.1 us -> 46.7 us  [reduce_all(): pl.pallas_call(reduce_kernel, name='reduce_all', out_shape=(jax.ShapeDtyp...]
where the time goes in v6:
time: 138 us
  Pallas kernels  136 us (99%)
    pallas_call x1, Pallas kernels, project(): pl.pallas_call(project_kernel, name='project', out_shape=(jax.ShapeDtypeS...  76.9 us
    pallas_call x1, Pallas kernels, reduce_all(): pl.pallas_call(reduce_kernel, name='reduce_all', out_shape=(jax.ShapeDtyp...  46.7 us
    pallas_call x1, Pallas kernels, attend(): pl.pallas_call(attend_kernel, name='attend', out_shape=(jax.ShapeDtypeStr...  10.3 us

profile of v6, /device:TPU:1, one launch (start us, length us, event | category | flops | bytes accessed | tf_op | source)
XLA Modules:
  0.0 137.6 jit_solution(13647043469671395562)
XLA Ops:
  0.7 0.1 add_multiply_fusion
  0.8 0.1 add_convert_fusion
  0.9 1.0 multiply_sine_fusion
  1.8 76.9 %project.1 = (bf16[128,4096]{1,0:T(8,128)(2,1)}, bf16[2,128,512]{2,1,0:T(8,128)(2,1)}, bf16[2,128,512]{2,1,0:T(8,128)(2,1)}, bf16[2,64,128,256]{3,2,1,0:T(8,128)...) custom-call(bf16[128,4096]{1,0:T(8,128)(2,1)} %x_ref.1, f32[1,4096]{1,0:T(1,128)} %bitcast.8, ...), custom_call_target="tpu_custom_call" | custom-call | tf_op jit(solution)/shard_map/project/pallas_call | solution.py:364
  78.7 10.3 %attend.1 = (bf16[2,128,512]{2,1,0:T(8,128)(2,1)}, bf16[2,128,512]{2,1,0:T(8,128)(2,1)}) custom-call(bf16[2,128,512]{2,1,0:T(8,128)(2,1)} %get-tuple-element.17.qx_ref, bf16[2,128,512]{2,1,0:T(8,128)(2,1)} %get-tuple-element.18.dox_ref, bf16[2,64,128,256]{3,2,1,0:T(8,128)(2,1)} %get-tuple-element.19.kvg_ref, s32[2,64,8,128]{3,2,1,0:T(8,128)} %get-tuple-element.20.idg_ref, ...), custom_call_target="tpu_custom_call" | custom-call | tf_op jit(solution)/shard_map/attend/pallas_call | solution.py:535
  89.1 46.7 %reduce_all.1 = (bf16[128,1024]{1,0:T(8,128)(2,1)}, f32[16,4096]{1,0:T(8,128)}, f32[16,1024]{1,0:T(8,128)}) custom-call(bf16[2,128,512]{2,1,0:T(8,128)(2,1)} %get-tuple-element.21.ox_ref, bf16[2,128,512]{2,1,0:T(8,128)(2,1)} %get-tuple-element.22.glx_ref, bf16[2,16,128]{2,1,0:T(8,128)(2,1)} %get-tuple-element.23.lowx_ref, ...), custom_call_target="tpu_custom_call" | custom-call | tf_op jit(solution)/shard_map/reduce_all/pallas_call | solution.py:676
  135.7 1.9 %hand_over.1 = (bf16[128,1024]{1,0:T(8,128)(2,1)}, f32[16,4096]{1,0:T(8,128)}, f32[16,1024]{1,0:T(8,128)}) custom-call(bf16[128,1024]{1,0:T(8,128)(2,1)} %get-tuple-element.25.a_ref, f32[16,4096]{1,0:T(8,128)} %get-tuple-element.26.b_ref, f32[16,1024]{1,0:T(8,128)} %get-tuple-element.27.c_ref), custom_call_target="tpu_custom_call" | custom-call | tf_op jit(solution)/shard_map/hand_over/pallas_call | solution.py:707
  (1 shorter events, 0.0 us)
